TPU v7x, 32 devices: a whole 2x2x4 slice. The times are simulated.
32 devices in a mesh: seq: 8 (over z, core), tp: 4 (over y, x).
Axes of the slice: x: 2, y: 2, z: 4, core: 2. Of those that a mesh axis runs over, the one named last changes fastest.
Arguments:
- tokens: bfloat16 [2048, 4608], P('seq', 'tp'), may hold values from -6 to 6
- attention_gain: float32 [4608], replicated, may hold values from 0.25 to 1.75
- query_weight: bfloat16 [4608, 4096], P(None, 'tp'), may hold values from -0.09375 to 0.09375
- key_weight: bfloat16 [4608, 2048], P(None, 'tp'), may hold values from -0.09375 to 0.09375
- value_weight: bfloat16 [4608, 2048], P(None, 'tp'), may hold values from -0.09375 to 0.09375
- output_weight: bfloat16 [4096, 4608], P('tp'), may hold values from -0.09375 to 0.09375
- post_gain: float32 [4608], replicated, may hold values from 0.25 to 1.75
- local_gain: float32 [4608], replicated, may hold values from 0.25 to 1.75
- local_query_weight: bfloat16 [4608, 4096], P(None, 'tp'), may hold values from -0.09375 to 0.09375
- local_key_weight: bfloat16 [4608, 2048], P(None, 'tp'), may hold values from -0.09375 to 0.09375
- local_value_weight: bfloat16 [4608, 2048], P(None, 'tp'), may hold values from -0.09375 to 0.09375
Outputs:
- hidden: bfloat16 [2048, 4608], P('seq', 'tp')
- local_heads: bfloat16 [2048, 4096], P('seq', 'tp')
All inputs are finite; a program needn't handle non-finite values.
Results may differ from a plain program's by a relative error of at most 0.02.
Values may be sent and summed in bfloat16 or wider, within the bound.
A program may use at most 128 MiB of HBM per device.

v0:
```python
import functools
import math

import jax
import jax.numpy as jnp
from jax import lax
from jax.experimental import pallas as pl
from jax.experimental.pallas import tpu as pltpu
from jax.sharding import PartitionSpec as P

D = 4608
HEADS = 32
HEAD_DIM = 128
WINDOW = 128

SOFT_CAP = 50.0
NORM_EPS = 1e-06
MESH = pl.DeviceIdType.MESH
VMEM = pltpu.VMEM
F32 = jnp.float32
BF16 = jnp.bfloat16
INNER = float(D // HEADS) ** (-0.5) / SOFT_CAP
OUTER = SOFT_CAP * math.log2(math.e)


def greet(peers):
    barrier = pltpu.get_barrier_semaphore()
    for peer in peers:
        pl.semaphore_signal(barrier, inc=1, device_id=peer, device_id_type=MESH)
    pl.semaphore_wait(barrier, len(peers))


def remote(source, target, send_sem, recv_sem, device):
    return pltpu.make_async_remote_copy(
        src_ref=source,
        dst_ref=target,
        send_sem=send_sem,
        recv_sem=recv_sem,
        device_id=device,
        device_id_type=MESH,
    )


def xor(index, bits):
    low, high = index % 2, index // 2
    if bits & 1:
        low = 1 - low
    if bits & 2:
        high = 1 - high
    return high * 2 + low


def gather_project_kernel(
    heads, kv_heads, x_ref, gain_ref, cos_ref, sin_ref, wq_ref, wk_ref, wv_ref,
    q_ref, kv_ref, buf, xg, w, acc, ss, send, recv, wsem,
):
    me = lax.axis_index("tp")
    rows, cols = x_ref.shape
    half = rows // 2
    owners = [xor(me, bits) for bits in range(4)]
    along_x, along_y = {"tp": owners[1]}, {"tp": owners[2]}
    qc, kc = heads * HEAD_DIM, kv_heads * HEAD_DIM
    total = qc + 2 * kc

    loads = []
    for slot in range(4):
        span = pl.ds(pl.multiple_of(owners[slot] * cols, cols), cols)
        parts = ((wq_ref, 0, qc), (wk_ref, qc, kc), (wv_ref, qc + kc, kc))
        group = []
        for which, (ref, begin, width) in enumerate(parts):
            copy = pltpu.make_async_copy(
                ref.at[span, :], w.at[slot, :, pl.ds(begin, width)], wsem.at[slot, which]
            )
            copy.start()
            group.append(copy)
        loads.append(group)

    greet([along_x, along_y])
    top, bottom = pl.ds(0, half), pl.ds(half, half)
    x_top = remote(x_ref.at[top], buf.at[0, top], send.at[0], recv.at[0], along_x)
    y_bottom = remote(x_ref.at[bottom], buf.at[1, bottom], send.at[1], recv.at[1], along_y)
    x_bottom = remote(x_ref.at[bottom], buf.at[0, bottom], send.at[2], recv.at[2], along_x)
    y_top = remote(x_ref.at[top], buf.at[1, top], send.at[3], recv.at[3], along_y)
    pass_y = remote(buf.at[0, top], buf.at[2, top], send.at[4], recv.at[4], along_y)
    pass_x = remote(buf.at[1, bottom], buf.at[2, bottom], send.at[5], recv.at[5], along_x)
    x_top.start()
    y_bottom.start()
    x_bottom.start()
    y_top.start()

    tile = 256 if total % 256 == 0 else 128
    step_rows = 64 if rows % 64 == 0 else rows

    def take(slot, source):
        gain_span = pl.ds(pl.multiple_of(owners[slot] * cols, cols), cols)

        def prepare(i, carry):
            part = pl.ds(pl.multiple_of(i * step_rows, step_rows), step_rows)
            wide = source[part, :].astype(F32)
            squares = jnp.sum(wide * wide, axis=-1, keepdims=True)
            spread = jnp.broadcast_to(squares, (step_rows, HEAD_DIM))
            if slot == 0:
                ss[part, :] = spread
            else:
                ss[part, :] += spread
            xg[part, :] = (wide * gain_ref[:, gain_span]).astype(BF16)
            return carry

        lax.fori_loop(0, rows // step_rows, prepare, 0)
        for copy in loads[slot]:
            copy.wait()

        def multiply(j, carry):
            span = pl.ds(pl.multiple_of(j * tile, tile), tile)
            product = jnp.dot(xg[...], w[slot, :, span], preferred_element_type=F32)
            if slot == 0:
                acc[:, span] = product
            else:
                acc[:, span] += product
            return carry

        lax.fori_loop(0, total // tile, multiply, 0)

    take(0, x_ref)
    x_top.wait_recv()
    pass_y.start()
    y_bottom.wait_recv()
    pass_x.start()
    x_bottom.wait_recv()
    take(1, buf.at[0])
    y_top.wait_recv()
    take(2, buf.at[1])
    pass_y.wait_recv()
    pass_x.wait_recv()
    take(3, buf.at[2])

    factor = lax.rsqrt(ss[...] * (1.0 / D) + NORM_EPS)

    def rotated(index):
        u = acc[:, pl.ds(index * HEAD_DIM, HEAD_DIM)] * factor
        return u * cos_ref[...] + pltpu.roll(u, HEAD_DIM // 2, 1) * sin_ref[...]

    for h in range(heads):
        q_ref[h] = rotated(h).astype(BF16)
    for h in range(kv_heads):
        kv_ref[0, h] = rotated(heads + h).astype(BF16)
        place = (heads + kv_heads + h) * HEAD_DIM
        kv_ref[1, h] = (acc[:, pl.ds(place, HEAD_DIM)] * factor).astype(BF16)
    for copy in (x_top, y_bottom, x_bottom, y_top, pass_y, pass_x):
        copy.wait_send()


def gather_project(x, gain, cos, sin, wq, wk, wv, collective_id):
    rows, cols = x.shape
    heads, kv_heads = wq.shape[1] // HEAD_DIM, wk.shape[1] // HEAD_DIM
    total = wq.shape[1] + 2 * wk.shape[1]
    vmem = pl.BlockSpec(memory_space=VMEM)
    hbm = pl.BlockSpec(memory_space=pl.ANY)
    return pl.pallas_call(
        functools.partial(gather_project_kernel, heads, kv_heads),
        out_shape=(
            jax.ShapeDtypeStruct((heads, rows, HEAD_DIM), BF16),
            jax.ShapeDtypeStruct((2, kv_heads, rows, HEAD_DIM), BF16),
        ),
        in_specs=[vmem] * 4 + [hbm] * 3,
        out_specs=(vmem, vmem),
        scratch_shapes=[
            VMEM((3, rows, cols), BF16),
            VMEM((rows, cols), BF16),
            VMEM((4, cols, total), BF16),
            VMEM((rows, total), F32),
            VMEM((rows, HEAD_DIM), F32),
            pltpu.SemaphoreType.DMA((6,)),
            pltpu.SemaphoreType.DMA((6,)),
            pltpu.SemaphoreType.DMA((4, 3)),
        ],
        compiler_params=pltpu.CompilerParams(
            collective_id=collective_id, has_side_effects=True, vmem_limit_bytes=48 * 2**20
        ),
        name=f"gather_project_{collective_id}",
    )(x, gain[None, :], cos, sin, wq, wk, wv)


def attend(q_ref, keys, values, acc, lsum, h, group, allowed, first, row_span=None):
    q = q_ref[pl.ds(h * group, group)]
    if row_span is not None:
        q = q[:, row_span[0] : row_span[1]]
    rows = q.shape[1]
    q = q.reshape(group * rows, HEAD_DIM)
    scores = lax.dot_general(q, keys, (((1,), (1,)), ((), ())), preferred_element_type=F32)
    weights = jnp.exp2(jnp.tanh(scores * INNER) * OUTER)
    if allowed is not None:
        count = keys.shape[0]
        row = lax.broadcasted_iota(jnp.int32, (rows, count), 0)
        col = lax.broadcasted_iota(jnp.int32, (rows, count), 1)
        mask = allowed(row, col)
        weights = jnp.concatenate(
            [jnp.where(mask, weights[g * rows : (g + 1) * rows], 0.0) for g in range(group)], axis=0
        )
    lanes = weights[:, :HEAD_DIM]
    for begin in range(HEAD_DIM, keys.shape[0], HEAD_DIM):
        lanes = lanes + weights[:, begin : begin + HEAD_DIM]
    product = jnp.dot(weights.astype(BF16), values, preferred_element_type=F32)
    lanes = lanes.reshape(group, rows, HEAD_DIM)
    product = product.reshape(group, rows, HEAD_DIM)
    heads = pl.ds(h * group, group)
    span = pl.ds(0, rows)
    if first:
        lsum[heads, span] = lanes
        acc[heads, span] = product
    else:
        lsum[heads, span] += lanes
        acc[heads, span] += product


def write_heads(o_ref, acc, lsum):
    for h in range(acc.shape[0]):
        denominator = jnp.sum(lsum[h], axis=-1, keepdims=True)
        o_ref[:, h * HEAD_DIM : (h + 1) * HEAD_DIM] = (acc[h] / denominator).astype(BF16)


def causal_kernel(levels, q_ref, kv_ref, o_ref, buf, acc, lsum, up_sem, side_sem, recv):
    s = lax.axis_index("seq")
    z, c = s // 2, s % 2
    mate = s + 1 - 2 * c
    kv_heads = kv_ref.shape[1]
    group = q_ref.shape[0] // kv_heads
    has_up, has_down = z < levels - 1, z > 0

    barrier = pltpu.get_barrier_semaphore()
    pl.semaphore_signal(barrier, inc=1, device_id={"seq": mate}, device_id_type=MESH)

    @pl.when(has_up)
    def _():
        pl.semaphore_signal(barrier, inc=1, device_id={"seq": s + 2}, device_id_type=MESH)

    @pl.when(has_down)
    def _():
        pl.semaphore_signal(barrier, inc=1, device_id={"seq": s - 2}, device_id_type=MESH)

    pl.semaphore_wait(barrier, 1 + has_up.astype(jnp.int32) + has_down.astype(jnp.int32))

    def up(owner, source):
        return remote(source, buf.at[owner], up_sem.at[owner], recv.at[owner], {"seq": s + 2})

    def side(owner, source):
        return remote(source, buf.at[owner], side_sem.at[owner], recv.at[owner], {"seq": mate})

    @pl.when(has_up)
    def _():
        up(s, kv_ref).start()

    @pl.when(c == 0)
    def _():
        side(s, kv_ref).start()

    def own(h, carry):
        attend(
            q_ref, kv_ref[0, h], kv_ref[1, h], acc, lsum, h, group,
            lambda row, col: col <= row, True,
        )
        return carry

    lax.fori_loop(0, kv_heads, own, 0)

    def visit(owner):
        def body(h, carry):
            attend(
                q_ref, buf[owner, 0, h], buf[owner, 1, h], acc, lsum, h, group, None, False
            )
            return carry

        lax.fori_loop(0, kv_heads, body, 0)

    @pl.when(c == 1)
    def _():
        side(s - 1, buf.at[s - 1]).wait_recv()
        visit(s - 1)

    def level(k, carry):
        owner, other = s - 2 * k, mate - 2 * k
        up(owner, buf.at[owner]).wait_recv()

        @pl.when(has_up)
        def _():
            up(owner, buf.at[owner]).start()

        side(owner, buf.at[owner]).start()
        visit(owner)
        side(other, buf.at[other]).wait_recv()
        visit(other)
        return carry

    lax.fori_loop(1, z + 1, level, 0)
    write_heads(o_ref, acc, lsum)

    @pl.when(has_up)
    def _():
        up(s, kv_ref).wait_send()

    @pl.when(c == 0)
    def _():
        side(s, kv_ref).wait_send()

    def drain(k, carry):
        owner = s - 2 * k

        @pl.when(has_up)
        def _():
            up(owner, buf.at[owner]).wait_send()

        side(owner, buf.at[owner]).wait_send()
        return carry

    lax.fori_loop(1, z + 1, drain, 0)


def causal_attention(q, kv, count, collective_id):
    heads, rows, _ = q.shape
    vmem = pl.BlockSpec(memory_space=VMEM)
    return pl.pallas_call(
        functools.partial(causal_kernel, count // 2),
        out_shape=jax.ShapeDtypeStruct((rows, heads * HEAD_DIM), BF16),
        in_specs=[vmem] * 2,
        out_specs=vmem,
        scratch_shapes=[
            VMEM((count,) + kv.shape, BF16),
            VMEM(q.shape, F32),
            VMEM(q.shape, F32),
            pltpu.SemaphoreType.DMA((count,)),
            pltpu.SemaphoreType.DMA((count,)),
            pltpu.SemaphoreType.DMA((count,)),
        ],
        compiler_params=pltpu.CompilerParams(
            collective_id=collective_id, has_side_effects=True, vmem_limit_bytes=32 * 2**20
        ),
        name="causal_attention",
    )(q, kv)


def front_kernel(
    levels, heads, kv_heads, x_ref, gain_ref, cos_ref, sin_ref, wq_ref, wk_ref, wv_ref,
    o_ref, buf, xg, w, acc, ss, q_all, kv_own, kv_buf, out, lsum,
    send, recv, wsem, up_sem, side_sem, kv_sem,
):
    me = lax.axis_index("tp")
    s = lax.axis_index("seq")
    z, c = s // 2, s % 2
    mate = s + 1 - 2 * c
    has_up, has_down = z < levels - 1, z > 0
    rows, cols = x_ref.shape
    half, quarter = rows // 2, rows // 4
    owners = [xor(me, bits) for bits in range(4)]
    along_x, along_y = {"tp": owners[1]}, {"tp": owners[2]}
    qc, kc = heads * HEAD_DIM, kv_heads * HEAD_DIM
    total = qc + 2 * kc
    group = heads // kv_heads

    loads = []
    for slot in range(4):
        span = pl.ds(pl.multiple_of(owners[slot] * cols, cols), cols)
        parts = ((wq_ref, 0, qc), (wk_ref, qc, kc), (wv_ref, qc + kc, kc))
        bundle = []
        for which, (ref, begin, width) in enumerate(parts):
            copy = pltpu.make_async_copy(
                ref.at[span, :], w.at[slot, :, pl.ds(begin, width)], wsem.at[slot, which]
            )
            copy.start()
            bundle.append(copy)
        loads.append(bundle)

    barrier = pltpu.get_barrier_semaphore()
    for peer in (along_x, along_y, {"seq": mate}):
        pl.semaphore_signal(barrier, inc=1, device_id=peer, device_id_type=MESH)

    @pl.when(has_up)
    def _():
        pl.semaphore_signal(barrier, inc=1, device_id={"seq": s + 2}, device_id_type=MESH)

    @pl.when(has_down)
    def _():
        pl.semaphore_signal(barrier, inc=1, device_id={"seq": s - 2}, device_id_type=MESH)

    pl.semaphore_wait(barrier, 3 + has_up.astype(jnp.int32) + has_down.astype(jnp.int32))

    moves = []
    for part in range(2):
        top, bottom = pl.ds(part * half, quarter), pl.ds(part * half + quarter, quarter)
        spec = (
            (x_ref.at[top], buf.at[0, top], along_x),
            (x_ref.at[bottom], buf.at[1, bottom], along_y),
            (x_ref.at[bottom], buf.at[0, bottom], along_x),
            (x_ref.at[top], buf.at[1, top], along_y),
            (buf.at[0, top], buf.at[2, top], along_y),
            (buf.at[1, bottom], buf.at[2, bottom], along_x),
        )
        moves.append(
            [
                remote(source, target, send.at[part * 6 + i], recv.at[part * 6 + i], device)
                for i, (source, target, device) in enumerate(spec)
            ]
        )

    def begin_gather(part):
        for i in range(4):
            moves[part][i].start()

    def pass_on(part):
        moves[part][0].wait_recv()
        moves[part][4].start()
        moves[part][1].wait_recv()
        moves[part][5].start()

    def up(owner, part, source):
        index = owner * 2 + part
        return remote(
            source, kv_buf.at[index], up_sem.at[index], kv_sem.at[index], {"seq": s + 2}
        )

    def side(owner, part, source):
        index = owner * 2 + part
        return remote(
            source, kv_buf.at[index], side_sem.at[index], kv_sem.at[index], {"seq": mate}
        )

    def arrive(owner, part):
        block = kv_buf.at[owner * 2 + part]
        up(owner, part, block).wait_recv()

        @pl.when(has_up)
        def _():
            up(owner, part, block).start()

        side(owner, part, block).start()

    tile = 256 if total % 256 == 0 else 128
    step_rows = 64 if half % 64 == 0 else half

    def take(slot, part, source):
        gain_span = pl.ds(pl.multiple_of(owners[slot] * cols, cols), cols)

        def prepare(i, carry):
            here = pl.ds(pl.multiple_of(i * step_rows, step_rows), step_rows)
            there = pl.ds(pl.multiple_of(part * half + i * step_rows, step_rows), step_rows)
            wide = source[there, :].astype(F32)
            squares = jnp.sum(wide * wide, axis=-1, keepdims=True)
            spread = jnp.broadcast_to(squares, (step_rows, HEAD_DIM))
            if slot == 0:
                ss[here, :] = spread
            else:
                ss[here, :] += spread
            xg[here, :] = (wide * gain_ref[:, gain_span]).astype(BF16)
            return carry

        lax.fori_loop(0, half // step_rows, prepare, 0)
        if part == 0:
            for copy in loads[slot]:
                copy.wait()

        def multiply(j, carry):
            span = pl.ds(pl.multiple_of(j * tile, tile), tile)
            product = jnp.dot(xg[...], w[slot, :, span], preferred_element_type=F32)
            if slot == 0:
                acc[:, span] = product
            else:
                acc[:, span] += product
            return carry

        lax.fori_loop(0, total // tile, multiply, 0)

    def finish_part(part):
        factor = lax.rsqrt(ss[...] * (1.0 / D) + NORM_EPS)
        span = pl.ds(part * half, half)

        def rotated(index):
            u = acc[:, pl.ds(index * HEAD_DIM, HEAD_DIM)] * factor
            turned = pltpu.roll(u, HEAD_DIM // 2, 1)
            return (u * cos_ref[span, :] + turned * sin_ref[span, :]).astype(BF16)

        for h in range(kv_heads):
            kv_own[part, 0, h] = rotated(heads + h)
            place = (heads + kv_heads + h) * HEAD_DIM
            kv_own[part, 1, h] = (acc[:, pl.ds(place, HEAD_DIM)] * factor).astype(BF16)
        for h in range(heads):
            q_all[h, span] = rotated(h)

        @pl.when(has_up)
        def _():
            up(s, part, kv_own.at[part]).start()

        @pl.when(c == 0)
        def _():
            side(s, part, kv_own.at[part]).start()

    begin_gather(0)
    take(0, 0, x_ref)
    pass_on(0)
    begin_gather(1)
    moves[0][2].wait_recv()
    take(1, 0, buf.at[0])
    moves[0][3].wait_recv()
    take(2, 0, buf.at[1])
    moves[0][4].wait_recv()
    moves[0][5].wait_recv()
    take(3, 0, buf.at[2])
    finish_part(0)
    pass_on(1)
    take(0, 1, x_ref)
    moves[1][2].wait_recv()
    take(1, 1, buf.at[0])
    moves[1][3].wait_recv()
    take(2, 1, buf.at[1])

    @pl.when(has_down)
    def _():
        arrive(s - 2, 0)

    moves[1][4].wait_recv()
    moves[1][5].wait_recv()
    take(3, 1, buf.at[2])
    finish_part(1)

    for part in range(2):
        shift = part * half

        def own(h, carry):
            attend(
                q_all, kv_own[part, 0, h], kv_own[part, 1, h], out, lsum, h, group,
                lambda row, col: col + shift <= row, part == 0,
            )
            return carry

        lax.fori_loop(0, kv_heads, own, 0)

    def visit(owner, part):
        index = owner * 2 + part

        def body(h, carry):
            attend(
                q_all, kv_buf[index, 0, h], kv_buf[index, 1, h], out, lsum, h, group, None, False
            )
            return carry

        lax.fori_loop(0, kv_heads, body, 0)

    @pl.when(z > 0)
    def _():
        arrive(s - 2, 1)

    @pl.when(c == 1)
    def _():
        for part in range(2):
            side(s - 1, part, kv_buf.at[(s - 1) * 2 + part]).wait_recv()
            visit(s - 1, part)

    def level(unit, carry):
        k, part = 1 + unit // 2, unit % 2
        owner, other = s - 2 * k, mate - 2 * k

        @pl.when(unit >= 2)
        def _():
            arrive(owner, part)

        visit(owner, part)
        side(other, part, kv_buf.at[other * 2 + part]).wait_recv()
        visit(other, part)
        return carry

    lax.fori_loop(0, 2 * z, level, 0)
    write_heads(o_ref, out, lsum)

    for part in range(2):
        for copy in moves[part]:
            copy.wait_send()

        @pl.when(has_up)
        def _():
            up(s, part, kv_own.at[part]).wait_send()

        @pl.when(c == 0)
        def _():
            side(s, part, kv_own.at[part]).wait_send()

    def drain(unit, carry):
        owner, part = s - 2 * (1 + unit // 2), unit % 2
        block = kv_buf.at[owner * 2 + part]

        @pl.when(has_up)
        def _():
            up(owner, part, block).wait_send()

        side(owner, part, block).wait_send()
        return carry

    lax.fori_loop(0, 2 * z, drain, 0)


def front(x, gain, cos, sin, wq, wk, wv, count, collective_id):
    rows, cols = x.shape
    half = rows // 2
    heads, kv_heads = wq.shape[1] // HEAD_DIM, wk.shape[1] // HEAD_DIM
    total = wq.shape[1] + 2 * wk.shape[1]
    vmem = pl.BlockSpec(memory_space=VMEM)
    hbm = pl.BlockSpec(memory_space=pl.ANY)
    return pl.pallas_call(
        functools.partial(front_kernel, count // 2, heads, kv_heads),
        out_shape=jax.ShapeDtypeStruct((rows, heads * HEAD_DIM), BF16),
        in_specs=[vmem] * 4 + [hbm] * 3,
        out_specs=vmem,
        scratch_shapes=[
            VMEM((3, rows, cols), BF16),
            VMEM((half, cols), BF16),
            VMEM((4, cols, total), BF16),
            VMEM((half, total), F32),
            VMEM((half, HEAD_DIM), F32),
            VMEM((heads, rows, HEAD_DIM), BF16),
            VMEM((2, 2, kv_heads, half, HEAD_DIM), BF16),
            VMEM((2 * count, 2, kv_heads, half, HEAD_DIM), BF16),
            VMEM((heads, rows, HEAD_DIM), F32),
            VMEM((heads, rows, HEAD_DIM), F32),
            pltpu.SemaphoreType.DMA((12,)),
            pltpu.SemaphoreType.DMA((12,)),
            pltpu.SemaphoreType.DMA((4, 3)),
            pltpu.SemaphoreType.DMA((2 * count,)),
            pltpu.SemaphoreType.DMA((2 * count,)),
            pltpu.SemaphoreType.DMA((2 * count,)),
        ],
        compiler_params=pltpu.CompilerParams(
            collective_id=collective_id, has_side_effects=True, vmem_limit_bytes=48 * 2**20
        ),
        name="front",
    )(x, gain[None, :], cos, sin, wq, wk, wv)


def output_kernel(
    a_ref, tok_ref, gain_ref, wo_ref, hidden_ref,
    wbuf, part, own, landed, passed, mine, stats, wsem, send, recv, ssend, srecv,
):
    me = lax.axis_index("tp")
    rows, cols = tok_ref.shape
    half = rows // 2
    owners = [xor(me, bits) for bits in range(4)]
    peers = [{"tp": owner} for owner in owners]
    order = (3, 1, 2, 0)
    loads = []
    for slot, bits in enumerate(order):
        span = pl.ds(pl.multiple_of(owners[bits] * cols, cols), cols)
        copy = pltpu.make_async_copy(wo_ref.at[:, span], wbuf.at[slot], wsem.at[slot])
        copy.start()
        loads.append(copy)
    greet(peers[1:])
    top, bottom = pl.ds(0, half), pl.ds(half, half)
    diag_x = remote(part.at[0, top], landed.at[0], send.at[0], recv.at[0], peers[1])
    diag_y = remote(part.at[0, bottom], landed.at[1], send.at[1], recv.at[1], peers[2])
    last_x_top = remote(part.at[1, top], landed.at[2], send.at[2], recv.at[2], peers[1])
    last_y_bottom = remote(part.at[2, bottom], landed.at[3], send.at[3], recv.at[3], peers[2])
    last_x_bottom = remote(passed.at[1], landed.at[4], send.at[4], recv.at[4], peers[1])
    last_y_top = remote(passed.at[0], landed.at[5], send.at[5], recv.at[5], peers[2])

    tile = 384 if cols % 384 == 0 else 128

    def product(slot, store):
        loads[slot].wait()

        def body(j, carry):
            span = pl.ds(pl.multiple_of(j * tile, tile), tile)
            store(span, jnp.dot(a_ref[...], wbuf[slot, :, span], preferred_element_type=F32))
            return carry

        lax.fori_loop(0, cols // tile, body, 0)

    def store_part(slot):
        def store(span, value):
            part[slot, :, span] = value.astype(BF16)

        return store

    def store_own(span, value):
        own[:, span] = value

    product(0, store_part(0))
    diag_x.start()
    diag_y.start()
    product(1, store_part(1))
    last_x_top.start()
    product(2, store_part(2))
    last_y_bottom.start()
    product(3, store_own)
    diag_x.wait_recv()
    passed[0] = (part[2, 0:half].astype(F32) + landed[0].astype(F32)).astype(BF16)
    last_y_top.start()
    diag_y.wait_recv()
    passed[1] = (part[1, half:rows].astype(F32) + landed[1].astype(F32)).astype(BF16)
    last_x_bottom.start()
    last_x_top.wait_recv()
    own[0:half] += landed[2].astype(F32)
    last_y_bottom.wait_recv()
    own[half:rows] += landed[3].astype(F32)
    last_y_top.wait_recv()
    own[0:half] += landed[5].astype(F32)
    last_x_bottom.wait_recv()
    own[half:rows] += landed[4].astype(F32)

    lanes = jnp.zeros((rows, HEAD_DIM), F32)
    for begin in range(0, cols, HEAD_DIM):
        piece = own[:, begin : begin + HEAD_DIM]
        lanes = lanes + piece * piece
    ones = jnp.ones((8, HEAD_DIM), F32)
    highest = lax.Precision.HIGHEST
    mine[...] = lax.dot_general(
        ones, lanes, (((1,), (1,)), ((), ())), precision=highest, preferred_element_type=F32
    )
    swaps = []
    for bits in (3, 1, 2):
        swap = remote(mine, stats.at[bits - 1], ssend.at[bits - 1], srecv.at[bits - 1], peers[bits])
        swap.start()
        swaps.append(swap)
    for swap in swaps:
        swap.wait_recv()
    summed = mine[...] + stats[0] + stats[1] + stats[2]
    column = lax.dot_general(
        summed, ones * 0.125, (((0,), (0,)), ((), ())), precision=highest,
        preferred_element_type=F32,
    )
    factor = lax.rsqrt(column * (1.0 / D) + NORM_EPS)
    span = pl.multiple_of(me * cols, cols)
    for begin in range(0, cols, HEAD_DIM):
        stop = begin + HEAD_DIM
        gain = gain_ref[:, pl.ds(pl.multiple_of(span + begin, HEAD_DIM), HEAD_DIM)]
        hidden_ref[:, begin:stop] = (
            tok_ref[:, begin:stop].astype(F32) + own[:, begin:stop] * factor * gain
        ).astype(BF16)
    for copy in (diag_x, diag_y, last_x_top, last_y_bottom, last_x_bottom, last_y_top, *swaps):
        copy.wait_send()


def output_project(attended, tokens, gain, wo, collective_id):
    rows, cols = tokens.shape
    depth = attended.shape[1]
    vmem = pl.BlockSpec(memory_space=VMEM)
    return pl.pallas_call(
        output_kernel,
        out_shape=jax.ShapeDtypeStruct((rows, cols), BF16),
        in_specs=[vmem] * 3 + [pl.BlockSpec(memory_space=pl.ANY)],
        out_specs=vmem,
        scratch_shapes=[
            VMEM((4, depth, cols), BF16),
            VMEM((3, rows, cols), BF16),
            VMEM((rows, cols), F32),
            VMEM((6, rows // 2, cols), BF16),
            VMEM((2, rows // 2, cols), BF16),
            VMEM((8, rows), F32),
            VMEM((3, 8, rows), F32),
            pltpu.SemaphoreType.DMA((4,)),
            pltpu.SemaphoreType.DMA((6,)),
            pltpu.SemaphoreType.DMA((6,)),
            pltpu.SemaphoreType.DMA((3,)),
            pltpu.SemaphoreType.DMA((3,)),
        ],
        compiler_params=pltpu.CompilerParams(
            collective_id=collective_id, has_side_effects=True, vmem_limit_bytes=40 * 2**20
        ),
        name="output_project",
    )(attended, tokens, gain[None, :], wo)


def window_kernel(count, q_ref, kv_ref, o_ref, tail, acc, lsum, send, recv):
    s = lax.axis_index("seq")
    kv_heads, rows = kv_ref.shape[1], kv_ref.shape[2]
    group = q_ref.shape[0] // kv_heads
    has_next, has_last = s < count - 1, s > 0
    barrier = pltpu.get_barrier_semaphore()

    @pl.when(has_next)
    def _():
        pl.semaphore_signal(barrier, inc=1, device_id={"seq": s + 1}, device_id_type=MESH)

    @pl.when(has_last)
    def _():
        pl.semaphore_signal(barrier, inc=1, device_id={"seq": s - 1}, device_id_type=MESH)

    pl.semaphore_wait(barrier, has_next.astype(jnp.int32) + has_last.astype(jnp.int32))
    copy = remote(
        kv_ref.at[:, :, pl.ds(rows - WINDOW, WINDOW), :], tail, send.at[0], recv.at[0],
        {"seq": s + 1},
    )

    @pl.when(has_next)
    def _():
        copy.start()

    def own(h, carry):
        attend(
            q_ref, kv_ref[0, h], kv_ref[1, h], acc, lsum, h, group,
            lambda row, col: (col <= row) & (row - col < WINDOW), True,
        )
        return carry

    lax.fori_loop(0, kv_heads, own, 0)

    @pl.when(has_last)
    def _():
        copy.wait_recv()

        def body(h, carry):
            attend(
                q_ref, tail[0, h], tail[1, h], acc, lsum, h, group,
                lambda row, col: col > row, False, (0, WINDOW),
            )
            return carry

        lax.fori_loop(0, kv_heads, body, 0)

    write_heads(o_ref, acc, lsum)

    @pl.when(has_next)
    def _():
        copy.wait_send()


def window_attention(q, kv, count, collective_id):
    heads, rows, _ = q.shape
    vmem = pl.BlockSpec(memory_space=VMEM)
    return pl.pallas_call(
        functools.partial(window_kernel, count),
        out_shape=jax.ShapeDtypeStruct((rows, heads * HEAD_DIM), BF16),
        in_specs=[vmem] * 2,
        out_specs=vmem,
        scratch_shapes=[
            VMEM((2, kv.shape[1], WINDOW, HEAD_DIM), BF16),
            VMEM(q.shape, F32),
            VMEM(q.shape, F32),
            pltpu.SemaphoreType.DMA((1,)),
            pltpu.SemaphoreType.DMA((1,)),
        ],
        compiler_params=pltpu.CompilerParams(
            collective_id=collective_id, has_side_effects=True, vmem_limit_bytes=24 * 2**20
        ),
        name="window_attention",
    )(q, kv)


def rms_scaled(values, weights):
    widened = values.astype(F32)
    factor = lax.rsqrt(jnp.mean(widened * widened, axis=-1, keepdims=True) + NORM_EPS)
    return widened * factor * weights


def plain_gather_project(x, gain, cos, sin, wq, wk, wv):
    full = lax.all_gather(x, "tp", axis=1, tiled=True)
    normed = rms_scaled(full, gain).astype(BF16)

    def heads_of(weight):
        product = jnp.dot(normed, weight, preferred_element_type=F32)
        return jnp.swapaxes(product.reshape(x.shape[0], -1, HEAD_DIM), 0, 1)

    def rotated(u):
        return (u * cos + jnp.roll(u, HEAD_DIM // 2, axis=-1) * sin).astype(BF16)

    keys, values = rotated(heads_of(wk)), heads_of(wv).astype(BF16)
    return rotated(heads_of(wq)), jnp.stack([keys, values])


def plain_output_project(attended, tokens, gain, wo):
    cols = tokens.shape[1]
    partial_sum = jnp.dot(attended, wo, preferred_element_type=F32).astype(BF16)
    summed = lax.psum(partial_sum, "tp").astype(F32)
    added = rms_scaled(summed, gain)
    mine = lax.dynamic_slice_in_dim(added, lax.axis_index("tp") * cols, cols, 1)
    return (tokens.astype(F32) + mine).astype(BF16)


def local(
    sizes,
    tokens,
    attention_gain,
    query_weight,
    key_weight,
    value_weight,
    output_weight,
    post_gain,
    local_gain,
    local_query_weight,
    local_key_weight,
    local_value_weight,
):
    seq, tp = sizes
    rows, cols = tokens.shape
    places = lax.axis_index("seq") * rows + lax.iota(jnp.int32, rows)
    halfway = HEAD_DIM // 2
    exponents = jnp.arange(halfway, dtype=F32) * (2.0 / HEAD_DIM)
    frequency = jnp.power(F32(10000.0), -exponents)
    angles = places.astype(F32)[:, None] * frequency[None, :]
    cosine, sine = jnp.cos(angles), jnp.sin(angles)
    cos = jnp.concatenate([cosine, cosine], axis=-1)
    sin = jnp.concatenate([-sine, sine], axis=-1)
    square = tp == 4 and cols % HEAD_DIM == 0

    def project(x, gain, wq, wk, wv, collective_id):
        if square:
            return gather_project(x, gain, cos, sin, wq, wk, wv, collective_id)
        return plain_gather_project(x, gain, cos, sin, wq, wk, wv)

    first = (tokens, attention_gain, cos, sin, query_weight, key_weight, value_weight)
    if square:
        attended = front(*first, seq, 0)
        hidden = output_project(attended, tokens, post_gain, output_weight, 2)
    else:
        attended = causal_attention(*plain_gather_project(*first), seq, 1)
        hidden = plain_output_project(attended, tokens, post_gain, output_weight)
    lq, lkv = project(
        hidden, local_gain, local_query_weight, local_key_weight, local_value_weight, 3
    )
    return hidden, window_attention(lq, lkv, seq, 4)


def solution(mesh):
    in_specs = (
        P("seq", "tp"),
        P(),
        P(None, "tp"),
        P(None, "tp"),
        P(None, "tp"),
        P("tp", None),
        P(),
        P(),
        P(None, "tp"),
        P(None, "tp"),
        P(None, "tp"),
    )
    out_specs = (P("seq", "tp"), P("seq", "tp"))
    sizes = (mesh.shape["seq"], mesh.shape["tp"])
    body = functools.partial(local, sizes)
    return jax.shard_map(body, mesh=mesh, in_specs=in_specs, out_specs=out_specs, check_vma=False)
```

profile of v0, /device:TPU:24, one launch (start us, length us, event | category | flops | bytes accessed | tf_op | source)
XLA Modules:
  0.0 130.8 jit_solution(11204726682055730003)
XLA Ops:
  0.7 0.5 fusion
  1.2 0.0 slice-start
  1.2 0.1 pad_maximum_fusion
  1.4 0.9 broadcast_in_dim.11.gain_ref
  2.3 0.0 copy-start
  2.3 2.6 %copy-done = bf16[4608,512]{1,0:T(8,128)(2,1)S(1)} copy-done((bf16[4608,512]{1,0:T(8,128)(2,1)S(1)}, bf16[4608,512]{1,0:T(8,128)(2,1)}, u32[]{:S(2)}) %copy-start) | copy-done | bytes 4718616
  4.8 0.0 copy-start.1
  4.8 1.1 copy-done.1
  5.9 0.0 copy-start.3
  5.9 0.0 slice-start.1
  5.9 0.0 slice-start.2
  5.9 0.0 copy-start.2
  5.9 59.6 %front.1.a_ref = bf16[256,1024]{1,0:T(8,128)(2,1)S(1)} custom-call(bf16[256,1152]{1,0:T(8,128)(2,1)S(1)} %copy-done.1, f32[1,4608]{1,0:T(1,128)S(1)} %broadcast_in_dim.11.gain_ref, f32[256,128]{1,0:T(8,128)S(1)} %get-tuple-element.9.cos_ref, f32[256,128]{1,0:T(8,128)S(1)} %get-tuple-element.10.sin_ref, bf16[4608,1024]{1,0:T(8,128)(2,1)} %wq_ref.2, ...), custom_call_target="tpu_custom_call" | custom-call | tf_op jit(solution)/shard_map/front/pallas_call | solution.py:605
  65.5 0.0 copy-done.3
  65.6 0.0 slice-done
  65.6 0.0 slice-done.1
  65.6 0.0 slice-done.2
  65.6 0.0 copy-done.2
  65.6 0.0 copy-start.4
  65.6 29.1 %output_project.1.x_ref = bf16[256,1152]{1,0:T(8,128)(2,1)S(1)} custom-call(bf16[256,1024]{1,0:T(8,128)(2,1)S(1)} %front.1.a_ref, bf16[256,1152]{1,0:T(8,128)(2,1)S(1)} %copy-done.2, f32[1,4608]{1,0:T(1,128)S(1)} %broadcast_in_dim.12.gain_ref, bf16[1024,4608]{1,0:T(8,128)(2,1)S(1)} %bitcast.1), custom_call_target="tpu_custom_call" | custom-call | tf_op jit(solution)/shard_map/output_project/pallas_call | solution.py:741
  94.8 0.0 copy-done.4
  94.8 26.9 %gather_project_3.1 = (bf16[8,256,128]{2,1,0:T(8,128)(2,1)S(1)}, bf16[2,4,256,128]{3,2,1,0:T(8,128)(2,1)S(1)}) custom-call(bf16[256,1152]{1,0:T(8,128)(2,1)S(1)} %output_project.1.x_ref, f32[1,4608]{1,0:T(1,128)S(1)} %broadcast_in_dim.13.gain_ref, f32[256,128]{1,0:T(8,128)S(1)} %get-tuple-element.9.cos_ref, f32[256,128]{1,0:T(8,128)S(1)} %get-tuple-element.10.sin_ref, ...), custom_call_target="tpu_custom_call" | custom-call | tf_op jit(solution)/shard_map/gather_project_3/pallas_call | solution.py:159
  121.8 7.5 %window_attention.1 = bf16[256,1024]{1,0:T(8,128)(2,1)S(1)} custom-call(bf16[8,256,128]{2,1,0:T(8,128)(2,1)S(1)} %get-tuple-element.4.q_ref, bf16[2,4,256,128]{3,2,1,0:T(8,128)(2,1)S(1)} %get-tuple-element.5.kv_ref), custom_call_target="tpu_custom_call" | custom-call | tf_op jit(solution)/shard_map/window_attention/pallas_call | solution.py:824
  129.2 0.8 copy.15
  130.1 0.8 copy.16
  (5 shorter events, 0.0 us)
Async XLA Ops:
  1.2 64.4 %slice-start = ((s8[9437184]{0:T(1024)(128)(4,1)}), s8[4194304]{0:T(1024)(128)(4,1)S(1)}, s32[]{:S(2)}) async-start(s8[9437184]{0:T(1024)(128)(4,1)} %bitcast), calls=%async_computation | async-start | bytes 8388608
  2.3 2.6 %copy-start = (bf16[4608,512]{1,0:T(8,128)(2,1)S(1)}, bf16[4608,512]{1,0:T(8,128)(2,1)}, u32[]{:S(2)}) copy-start(bf16[4608,512]{1,0:T(8,128)(2,1)} %wk_ref.2) | copy-start | bytes 14155780
  4.8 1.1 copy-start.1
  5.9 59.7 %copy-start.3 = (f32[4608]{0:T(1024)S(1)}, f32[4608]{0:T(1024)}, u32[]{:S(2)}) copy-start(f32[4608]{0:T(1024)} %param.17) | copy-start | bytes 55300
  5.9 59.7 %slice-start.1 = ((s8[9437184]{0:T(1024)(128)(4,1)}), s8[4194304]{0:T(1024)(128)(4,1)S(1)}, s32[]{:S(2)}) async-start(s8[9437184]{0:T(1024)(128)(4,1)} %bitcast), calls=%async_computation.1 | async-start | bytes 8388608
  5.9 59.7 %slice-start.2 = ((s8[9437184]{0:T(1024)(128)(4,1)}), s8[1048576]{0:T(1024)(128)(4,1)S(1)}, s32[]{:S(2)}) async-start(s8[9437184]{0:T(1024)(128)(4,1)} %bitcast), calls=%async_computation.2 | async-start | bytes 2097152
  5.9 59.7 %copy-start.2 = (bf16[256,1152]{1,0:T(8,128)(2,1)S(1)}, bf16[256,1152]{1,0:T(8,128)(2,1)}, u32[]{:S(2)}) copy-start(bf16[256,1152]{1,0:T(8,128)(2,1)} %tok_ref.1) | copy-start | bytes 1769476
  65.6 29.2 %copy-start.4 = (f32[4608]{0:T(1024)S(1)}, f32[4608]{0:T(1024)}, u32[]{:S(2)}) copy-start(f32[4608]{0:T(1024)} %param.18) | copy-start | bytes 55300
where the time goes:
time: 131 us
  Pallas kernels  123 us (94%)
  local copies, waits for them, and re-layouts  6.18 us (5%)
    pallas_call x1, Pallas kernels, front(): pl.pallas_call(functools.partial(front_kernel, count // 2, heads, kv_head...  59.6 us
    pallas_call x1, Pallas kernels, output_project(): pl.pallas_call(output_kernel, out_shape=jax.ShapeDtypeStruct((rows, cols)...  29.1 us
    pallas_call x1, Pallas kernels, gather_project(): pl.pallas_call(functools.partial(gather_project_kernel, heads, kv_heads),...  26.9 us
    pallas_call x1, Pallas kernels, window_attention(): pl.pallas_call(functools.partial(window_kernel, count), out_shape=jax.Sha...  7.48 us
    unnamed x18, local copies, waits for them, and re-layouts  5.26 us

commit v1 on v0

v1 whole, which is shorter than its diff:
```python
import functools
import math

import jax
import jax.numpy as jnp
from jax import lax
from jax.experimental import pallas as pl
from jax.experimental.pallas import tpu as pltpu
from jax.sharding import PartitionSpec as P

D = 4608
HEADS = 32
HEAD_DIM = 128
WINDOW = 128

SOFT_CAP = 50.0
NORM_EPS = 1e-06
MESH = pl.DeviceIdType.MESH
VMEM = pltpu.VMEM
F32 = jnp.float32
BF16 = jnp.bfloat16
PARTS = 4
INNER = float(D // HEADS) ** (-0.5) / SOFT_CAP
OUTER = SOFT_CAP * math.log2(math.e)


def greet(peers):
    barrier = pltpu.get_barrier_semaphore()
    for peer in peers:
        pl.semaphore_signal(barrier, inc=1, device_id=peer, device_id_type=MESH)
    pl.semaphore_wait(barrier, len(peers))


def remote(source, target, send_sem, recv_sem, device):
    return pltpu.make_async_remote_copy(
        src_ref=source,
        dst_ref=target,
        send_sem=send_sem,
        recv_sem=recv_sem,
        device_id=device,
        device_id_type=MESH,
    )


def xor(index, bits):
    low, high = index % 2, index // 2
    if bits & 1:
        low = 1 - low
    if bits & 2:
        high = 1 - high
    return high * 2 + low


def attend(q_ref, keys, values, acc, lsum, h, group, allowed, first, row_span=None):
    q = q_ref[pl.ds(h * group, group)]
    if row_span is not None:
        q = q[:, row_span[0] : row_span[1]]
    rows = q.shape[1]
    q = q.reshape(group * rows, HEAD_DIM)
    scores = lax.dot_general(q, keys, (((1,), (1,)), ((), ())), preferred_element_type=F32)
    weights = jnp.exp2(jnp.tanh(scores * INNER) * OUTER)
    if allowed is not None:
        count = keys.shape[0]
        row = lax.broadcasted_iota(jnp.int32, (rows, count), 0)
        col = lax.broadcasted_iota(jnp.int32, (rows, count), 1)
        mask = allowed(row, col)
        weights = jnp.concatenate(
            [jnp.where(mask, weights[g * rows : (g + 1) * rows], 0.0) for g in range(group)], axis=0
        )
    lanes = weights[:, :HEAD_DIM]
    for begin in range(HEAD_DIM, keys.shape[0], HEAD_DIM):
        lanes = lanes + weights[:, begin : begin + HEAD_DIM]
    product = jnp.dot(weights.astype(BF16), values, preferred_element_type=F32)
    lanes = lanes.reshape(group, rows, HEAD_DIM)
    product = product.reshape(group, rows, HEAD_DIM)
    heads = pl.ds(h * group, group)
    span = pl.ds(0, rows)
    if first:
        lsum[heads, span] = lanes
        acc[heads, span] = product
    else:
        lsum[heads, span] += lanes
        acc[heads, span] += product


def write_heads(o_ref, acc, lsum):
    for h in range(acc.shape[0]):
        denominator = jnp.sum(lsum[h], axis=-1, keepdims=True)
        o_ref[:, h * HEAD_DIM : (h + 1) * HEAD_DIM] = (acc[h] / denominator).astype(BF16)


def causal_kernel(levels, q_ref, kv_ref, o_ref, buf, acc, lsum, up_sem, side_sem, recv):
    s = lax.axis_index("seq")
    z, c = s // 2, s % 2
    mate = s + 1 - 2 * c
    kv_heads = kv_ref.shape[1]
    group = q_ref.shape[0] // kv_heads
    has_up, has_down = z < levels - 1, z > 0

    barrier = pltpu.get_barrier_semaphore()
    pl.semaphore_signal(barrier, inc=1, device_id={"seq": mate}, device_id_type=MESH)

    @pl.when(has_up)
    def _():
        pl.semaphore_signal(barrier, inc=1, device_id={"seq": s + 2}, device_id_type=MESH)

    @pl.when(has_down)
    def _():
        pl.semaphore_signal(barrier, inc=1, device_id={"seq": s - 2}, device_id_type=MESH)

    pl.semaphore_wait(barrier, 1 + has_up.astype(jnp.int32) + has_down.astype(jnp.int32))

    def up(owner, source):
        return remote(source, buf.at[owner], up_sem.at[owner], recv.at[owner], {"seq": s + 2})

    def side(owner, source):
        return remote(source, buf.at[owner], side_sem.at[owner], recv.at[owner], {"seq": mate})

    @pl.when(has_up)
    def _():
        up(s, kv_ref).start()

    @pl.when(c == 0)
    def _():
        side(s, kv_ref).start()

    def own(h, carry):
        attend(
            q_ref, kv_ref[0, h], kv_ref[1, h], acc, lsum, h, group,
            lambda row, col: col <= row, True,
        )
        return carry

    lax.fori_loop(0, kv_heads, own, 0)

    def visit(owner):
        def body(h, carry):
            attend(
                q_ref, buf[owner, 0, h], buf[owner, 1, h], acc, lsum, h, group, None, False
            )
            return carry

        lax.fori_loop(0, kv_heads, body, 0)

    @pl.when(c == 1)
    def _():
        side(s - 1, buf.at[s - 1]).wait_recv()
        visit(s - 1)

    def level(k, carry):
        owner, other = s - 2 * k, mate - 2 * k
        up(owner, buf.at[owner]).wait_recv()

        @pl.when(has_up)
        def _():
            up(owner, buf.at[owner]).start()

        side(owner, buf.at[owner]).start()
        visit(owner)
        side(other, buf.at[other]).wait_recv()
        visit(other)
        return carry

    lax.fori_loop(1, z + 1, level, 0)
    write_heads(o_ref, acc, lsum)

    @pl.when(has_up)
    def _():
        up(s, kv_ref).wait_send()

    @pl.when(c == 0)
    def _():
        side(s, kv_ref).wait_send()

    def drain(k, carry):
        owner = s - 2 * k

        @pl.when(has_up)
        def _():
            up(owner, buf.at[owner]).wait_send()

        side(owner, buf.at[owner]).wait_send()
        return carry

    lax.fori_loop(1, z + 1, drain, 0)


def causal_attention(q, kv, count, collective_id):
    heads, rows, _ = q.shape
    vmem = pl.BlockSpec(memory_space=VMEM)
    return pl.pallas_call(
        functools.partial(causal_kernel, count // 2),
        out_shape=jax.ShapeDtypeStruct((rows, heads * HEAD_DIM), BF16),
        in_specs=[vmem] * 2,
        out_specs=vmem,
        scratch_shapes=[
            VMEM((count,) + kv.shape, BF16),
            VMEM(q.shape, F32),
            VMEM(q.shape, F32),
            pltpu.SemaphoreType.DMA((count,)),
            pltpu.SemaphoreType.DMA((count,)),
            pltpu.SemaphoreType.DMA((count,)),
        ],
        compiler_params=pltpu.CompilerParams(
            collective_id=collective_id, has_side_effects=True, vmem_limit_bytes=32 * 2**20
        ),
        name="causal_attention",
    )(q, kv)


def window_kernel(count, q_ref, kv_ref, o_ref, tail, acc, lsum, send, recv):
    s = lax.axis_index("seq")
    kv_heads, rows = kv_ref.shape[1], kv_ref.shape[2]
    group = q_ref.shape[0] // kv_heads
    has_next, has_last = s < count - 1, s > 0
    barrier = pltpu.get_barrier_semaphore()

    @pl.when(has_next)
    def _():
        pl.semaphore_signal(barrier, inc=1, device_id={"seq": s + 1}, device_id_type=MESH)

    @pl.when(has_last)
    def _():
        pl.semaphore_signal(barrier, inc=1, device_id={"seq": s - 1}, device_id_type=MESH)

    pl.semaphore_wait(barrier, has_next.astype(jnp.int32) + has_last.astype(jnp.int32))
    copy = remote(
        kv_ref.at[:, :, pl.ds(rows - WINDOW, WINDOW), :], tail, send.at[0], recv.at[0],
        {"seq": s + 1},
    )

    @pl.when(has_next)
    def _():
        copy.start()

    def own(h, carry):
        attend(
            q_ref, kv_ref[0, h], kv_ref[1, h], acc, lsum, h, group,
            lambda row, col: (col <= row) & (row - col < WINDOW), True,
        )
        return carry

    lax.fori_loop(0, kv_heads, own, 0)

    @pl.when(has_last)
    def _():
        copy.wait_recv()

        def body(h, carry):
            attend(
                q_ref, tail[0, h], tail[1, h], acc, lsum, h, group,
                lambda row, col: col > row, False, (0, WINDOW),
            )
            return carry

        lax.fori_loop(0, kv_heads, body, 0)

    write_heads(o_ref, acc, lsum)

    @pl.when(has_next)
    def _():
        copy.wait_send()


def window_attention(q, kv, count, collective_id):
    heads, rows, _ = q.shape
    vmem = pl.BlockSpec(memory_space=VMEM)
    return pl.pallas_call(
        functools.partial(window_kernel, count),
        out_shape=jax.ShapeDtypeStruct((rows, heads * HEAD_DIM), BF16),
        in_specs=[vmem] * 2,
        out_specs=vmem,
        scratch_shapes=[
            VMEM((2, kv.shape[1], WINDOW, HEAD_DIM), BF16),
            VMEM(q.shape, F32),
            VMEM(q.shape, F32),
            pltpu.SemaphoreType.DMA((1,)),
            pltpu.SemaphoreType.DMA((1,)),
        ],
        compiler_params=pltpu.CompilerParams(
            collective_id=collective_id, has_side_effects=True, vmem_limit_bytes=24 * 2**20
        ),
        name="window_attention",
    )(q, kv)


def fused_kernel(
    levels, heads, kv_heads,
    x_hbm, gain1_hbm, gain2_hbm, gain3_hbm, cos_ref, sin_ref,
    wq_hbm, wk_hbm, wv_hbm, wo_hbm, lwq_hbm, lwk_hbm, lwv_hbm,
    hidden_ref, o_ref,
    buf, w, wo, gains, xg, acc, ss, q_all, kv_buf, out, lsum, att,
    terms, own, landed, passed, proj, mine, stats, kv2,
    x_sem, gain_sem, w_sem, wo_sem, ag_send, ag_recv, up_sem, side_sem, kv_sem,
    rs_send, rs_recv, st_send, st_recv, tail_sem,
):
    me = lax.axis_index("tp")
    s = lax.axis_index("seq")
    z, c = s // 2, s % 2
    mate = s + 1 - 2 * c
    has_up, has_down = z < levels - 1, z > 0
    next_row, prev_row = s < 2 * levels - 1, s > 0
    rows, cols = hidden_ref.shape
    chunk_rows, half_rows = rows // PARTS, rows // PARTS // 2
    block, half = rows // 2, rows // 4
    chunks = cols // HEAD_DIM
    owners = [xor(me, bits) for bits in range(4)]
    peers = [{"tp": owner} for owner in owners]
    along_x, along_y = peers[1], peers[2]
    qc, kc = heads * HEAD_DIM, kv_heads * HEAD_DIM
    kvc = 2 * kc
    group = heads // kv_heads

    x_loads = []
    for part in range(PARTS):
        span = pl.ds(part * chunk_rows, chunk_rows)
        copy = pltpu.make_async_copy(x_hbm.at[span], buf.at[0, span], x_sem.at[part])
        copy.start()
        x_loads.append(copy)
    gain_loads = []
    for i, ref in enumerate((gain1_hbm, gain2_hbm, gain3_hbm)):
        copy = pltpu.make_async_copy(ref, gains.at[i], gain_sem.at[i])
        copy.start()
        gain_loads.append(copy)

    def weight_loads(key, value, query):
        loads = []
        for slot in range(4):
            span = pl.ds(pl.multiple_of(owners[slot] * cols, cols), cols)
            spec = ((key, 0, kc), (value, kc, kc), (query, kvc, qc))
            loads.append(
                [
                    pltpu.make_async_copy(
                        ref.at[span, :], w.at[slot, :, pl.ds(begin, width)], w_sem.at[slot, i]
                    )
                    for i, (ref, begin, width) in enumerate(spec)
                ]
            )
        return loads

    first_loads = weight_loads(wk_hbm, wv_hbm, wq_hbm)
    for bundle in first_loads:
        for copy in bundle:
            copy.start()
    wo_loads = []
    for bits in (3, 1, 2, 0):
        span = pl.ds(pl.multiple_of(owners[bits] * cols, cols), cols)
        copy = pltpu.make_async_copy(wo_hbm.at[:, span], wo.at[bits], wo_sem.at[bits])
        copy.start()
        wo_loads.append(copy)

    barrier = pltpu.get_barrier_semaphore()
    for peer in (*peers[1:], {"seq": mate}):
        pl.semaphore_signal(barrier, inc=1, device_id=peer, device_id_type=MESH)

    @pl.when(has_up)
    def _():
        pl.semaphore_signal(barrier, inc=1, device_id={"seq": s + 2}, device_id_type=MESH)

    @pl.when(has_down)
    def _():
        pl.semaphore_signal(barrier, inc=1, device_id={"seq": s - 2}, device_id_type=MESH)

    @pl.when(has_up & (c == 1))
    def _():
        pl.semaphore_signal(barrier, inc=1, device_id={"seq": s + 1}, device_id_type=MESH)

    @pl.when(has_down & (c == 0))
    def _():
        pl.semaphore_signal(barrier, inc=1, device_id={"seq": s - 1}, device_id_type=MESH)

    far = (has_up & (c == 1)) | (has_down & (c == 0))
    pl.semaphore_wait(
        barrier,
        4 + has_up.astype(jnp.int32) + has_down.astype(jnp.int32) + far.astype(jnp.int32),
    )

    def gather_moves(store, first, count, part, base):
        begin = pl.multiple_of(part * count, count)
        top, bottom = pl.ds(begin, count // 2), pl.ds(begin + count // 2, count // 2)
        spec = (
            (store.at[0, top], store.at[1, top], along_x),
            (store.at[0, bottom], store.at[2, bottom], along_y),
            (store.at[0, bottom], store.at[1, bottom], along_x),
            (store.at[0, top], store.at[2, top], along_y),
            (store.at[1, top], store.at[3, top], along_y),
            (store.at[2, bottom], store.at[3, bottom], along_x),
        )
        at = first + part * 6 + base
        return [
            remote(source, target, ag_send.at[at + i], ag_recv.at[at + i], device)
            for i, (source, target, device) in enumerate(spec)
        ]

    def moves(part):
        return gather_moves(buf, 0, chunk_rows, part, 0)

    def moves2(part):
        return gather_moves(proj, 6 * PARTS, block, part, 0)

    def kv_part(owner, part):
        return kv_buf.at[owner, :, :, pl.ds(pl.multiple_of(part * chunk_rows, chunk_rows), chunk_rows)]

    def up(owner, part):
        at, ref = owner * PARTS + part, kv_part(owner, part)
        return remote(ref, ref, up_sem.at[at], kv_sem.at[at], {"seq": s + 2})

    def side(owner, part):
        at, ref = owner * PARTS + part, kv_part(owner, part)
        return remote(ref, ref, side_sem.at[at], kv_sem.at[at], {"seq": mate})

    def arrive(owner, part):
        up(owner, part).wait_recv()

        @pl.when(has_up)
        def _():
            up(owner, part).start()

        side(owner, part).start()

    def multiply(slot, count, begin, width, fresh):
        product = jnp.dot(
            xg[0:count, :], w[slot, :, begin : begin + width], preferred_element_type=F32
        )
        if fresh:
            acc[0:count, begin : begin + width] = product
        else:
            acc[0:count, begin : begin + width] += product

    def gain_row(which, slot, j):
        return gains[which, pl.ds(owners[slot] * chunks + j, 1), :]

    def prepare(slot, part):
        here = pl.ds(pl.multiple_of(part * chunk_rows, chunk_rows), chunk_rows)
        squares = None
        for j in range(chunks):
            lanes = slice(j * HEAD_DIM, (j + 1) * HEAD_DIM)
            wide = buf[slot, here, lanes].astype(F32)
            squares = wide * wide if squares is None else squares + wide * wide
            xg[0:chunk_rows, lanes] = (wide * gain_row(0, slot, j)).astype(BF16)
        if slot == 0:
            ss[0:chunk_rows, :] = squares
        else:
            ss[0:chunk_rows, :] += squares

    def row_factor(count):
        total = jnp.sum(ss[0:count, :], axis=-1, keepdims=True)
        return lax.rsqrt(jnp.broadcast_to(total, (count, HEAD_DIM)) * (1.0 / D) + NORM_EPS)

    def rotated(begin, count, factor, span):
        u = acc[0:count, begin : begin + HEAD_DIM] * factor
        turned = pltpu.roll(u, HEAD_DIM // 2, 1)
        return (u * cos_ref[span, :] + turned * sin_ref[span, :]).astype(BF16)

    for copy in x_loads[:1]:
        copy.wait()
    for copy in moves(0)[:4]:
        copy.start()
    for copy in x_loads[1:]:
        copy.wait()
    for copy in gain_loads:
        copy.wait()

    def first_part(part, carry):
        def take(slot):
            prepare(slot, part)

            @pl.when(part == 0)
            def _():
                for copy in first_loads[slot]:
                    copy.wait()

            multiply(slot, chunk_rows, 0, kvc, slot == 0)

        sends = moves(part)
        take(0)
        multiply(0, chunk_rows, kvc, qc, True)
        sends[0].wait_recv()
        sends[4].start()
        sends[1].wait_recv()
        sends[5].start()

        @pl.when(part < PARTS - 1)
        def _():
            for copy in moves(part + 1)[:4]:
                copy.start()

        sends[2].wait_recv()
        take(1)
        multiply(1, chunk_rows, kvc, qc, False)
        sends[3].wait_recv()
        take(2)
        multiply(2, chunk_rows, kvc, qc, False)

        def forward(k, carry):
            @pl.when(part >= k)
            def _():
                arrive(s - 2 * k, part - k)

            return carry

        @pl.when(has_up)
        def _():
            lax.fori_loop(1, z + 1, forward, 0)

        sends[4].wait_recv()
        sends[5].wait_recv()
        take(3)
        span = pl.ds(pl.multiple_of(part * chunk_rows, chunk_rows), chunk_rows)
        factor = row_factor(chunk_rows)
        for h in range(kv_heads):
            kv_buf[s, 0, h, span, :] = rotated(h * HEAD_DIM, chunk_rows, factor, span)
            place = kc + h * HEAD_DIM
            kv_buf[s, 1, h, span, :] = (
                acc[0:chunk_rows, place : place + HEAD_DIM] * factor
            ).astype(BF16)

        @pl.when(has_up)
        def _():
            up(s, part).start()

        @pl.when(c == 0)
        def _():
            side(s, part).start()

        multiply(3, chunk_rows, kvc, qc, False)
        for h in range(heads):
            q_all[h, span, :] = rotated(kvc + h * HEAD_DIM, chunk_rows, factor, span)
        return carry

    lax.fori_loop(0, PARTS, first_part, 0)

    second_loads = weight_loads(lwk_hbm, lwv_hbm, lwq_hbm)
    for bundle in second_loads:
        for copy in bundle:
            copy.start()

    for h in range(kv_heads):
        attend(
            q_all, kv_buf[s, 0, h], kv_buf[s, 1, h], out, lsum, h, group,
            lambda row, col: col <= row, True,
        )

    def visit(owner):
        for h in range(kv_heads):
            attend(
                q_all, kv_buf[owner, 0, h], kv_buf[owner, 1, h], out, lsum, h, group, None, False
            )

    @pl.when(c == 1)
    def _():
        for part in range(PARTS):
            side(s - 1, part).wait_recv()
        visit(s - 1)

    def turn(r, carry):
        def level(k, carry):
            part = r - k

            @pl.when((part >= 0) & (part < PARTS))
            def _():
                owner, other = s - 2 * k, mate - 2 * k

                @pl.when((r >= PARTS) | (z == levels - 1))
                def _():
                    arrive(owner, part)

                @pl.when(part == PARTS - 1)
                def _():
                    def both(j, carry):
                        @pl.when(j == 1)
                        def _():
                            for p in range(PARTS):
                                side(other, p).wait_recv()

                        visit(owner + j * (other - owner))
                        return carry

                    lax.fori_loop(0, 2, both, 0)

            return carry

        lax.fori_loop(1, z + 1, level, 0)
        return carry

    lax.fori_loop(1, PARTS + z, turn, 0)
    write_heads(att, out, lsum)

    def reduce_moves(part):
        base = part * block
        top, bottom = pl.ds(base, half), pl.ds(base + half, half)
        spec = (
            (terms.at[2, top], along_x),
            (terms.at[2, bottom], along_y),
            (terms.at[0, top], along_x),
            (terms.at[1, bottom], along_y),
            (passed.at[part, 1], along_x),
            (passed.at[part, 0], along_y),
        )
        return [
            remote(
                source, landed.at[part, i], rs_send.at[part * 6 + i], rs_recv.at[part * 6 + i], device
            )
            for i, (source, device) in enumerate(spec)
        ]

    def product(bits, part):
        span = slice(part * block, (part + 1) * block)
        value = jnp.dot(att[span, :], wo[bits], preferred_element_type=F32)
        if bits == 0:
            own[span, :] = value
        else:
            terms[bits - 1, span, :] = value.astype(BF16)

    def pass_on(part):
        copies = reduce_moves(part)
        base = part * block
        copies[0].wait_recv()
        passed[part, 0] = (
            terms[1, base : base + half].astype(F32) + landed[part, 0].astype(F32)
        ).astype(BF16)
        copies[5].start()
        copies[1].wait_recv()
        passed[part, 1] = (
            terms[0, base + half : base + block].astype(F32) + landed[part, 1].astype(F32)
        ).astype(BF16)
        copies[4].start()

    ones = jnp.ones((8, HEAD_DIM), F32)
    highest = lax.Precision.HIGHEST

    def swaps(part):
        return [
            remote(
                mine.at[part], stats.at[part, bits - 1],
                st_send.at[part * 3 + bits - 1], st_recv.at[part * 3 + bits - 1], peers[bits],
            )
            for bits in (3, 1, 2)
        ]

    def finalize(part):
        copies = reduce_moves(part)
        for i in (2, 3, 5, 4):
            copies[i].wait_recv()
        base = part * block
        span = slice(base, base + block)
        lanes = None
        for j in range(chunks):
            cut = slice(j * HEAD_DIM, (j + 1) * HEAD_DIM)
            above = landed[part, 2, :, cut].astype(F32) + landed[part, 5, :, cut].astype(F32)
            below = landed[part, 3, :, cut].astype(F32) + landed[part, 4, :, cut].astype(F32)
            value = own[span, cut] + jnp.concatenate([above, below], axis=0)
            own[span, cut] = value
            proj[0, span, cut] = value.astype(BF16)
            lanes = value * value if lanes is None else lanes + value * value
        for copy in moves2(part)[:2]:
            copy.start()
        mine[part] = lax.dot_general(
            ones, lanes, (((1,), (1,)), ((), ())), precision=highest, preferred_element_type=F32
        )
        for swap in swaps(part):
            swap.start()
        for copy in moves2(part)[2:4]:
            copy.start()

    def forward_rows(part):
        copies = moves2(part)
        copies[0].wait_recv()
        copies[4].start()
        copies[1].wait_recv()
        copies[5].start()

    def post_factor(part):
        for swap in swaps(part):
            swap.wait_recv()
        summed = mine[part] + stats[part, 0] + stats[part, 1] + stats[part, 2]
        column = lax.dot_general(
            summed, ones * 0.125, (((0,), (0,)), ((), ())), precision=highest,
            preferred_element_type=F32,
        )
        return lax.rsqrt(column * (1.0 / D) + NORM_EPS)

    def take2(slot, part, factor):
        span = slice(part * block, (part + 1) * block)
        squares = None
        for j in range(chunks):
            cut = slice(j * HEAD_DIM, (j + 1) * HEAD_DIM)
            summed = own[span, cut] if slot == 0 else proj[slot, span, cut].astype(F32)
            added = buf[slot, span, cut].astype(F32) + summed * factor * gain_row(1, slot, j)
            rounded = added.astype(BF16)
            if slot == 0:
                hidden_ref[span, cut] = rounded
            wide = rounded.astype(F32)
            squares = wide * wide if squares is None else squares + wide * wide
            xg[:, cut] = (wide * gain_row(2, slot, j)).astype(BF16)
        if slot == 0:
            ss[...] = squares
        else:
            ss[...] += squares
        if part == 1:
            for copy in second_loads[slot]:
                copy.wait()
        multiply(slot, block, 0, kvc, slot == 0)
        multiply(slot, block, kvc, qc, slot == 0)

    def finish2(part):
        span = pl.ds(part * block, block)
        place_rows = pl.ds(WINDOW + part * block, block)
        factor = row_factor(block)
        for h in range(kv_heads):
            kv2[0, h, place_rows, :] = rotated(h * HEAD_DIM, block, factor, span)
            place = kc + h * HEAD_DIM
            kv2[1, h, place_rows, :] = (acc[:, place : place + HEAD_DIM] * factor).astype(BF16)
        for h in range(heads):
            q_all[h, span, :] = rotated(kvc + h * HEAD_DIM, block, factor, span)

    tail = remote(
        kv2.at[:, :, pl.ds(rows, WINDOW)], kv2.at[:, :, pl.ds(0, WINDOW)],
        tail_sem.at[0], tail_sem.at[1], {"seq": s + 1},
    )

    for copy in wo_loads:
        copy.wait()
    late, soon = 0, 1
    copies = reduce_moves(soon)
    product(3, soon)
    copies[0].start()
    copies[1].start()
    product(1, soon)
    copies[2].start()
    product(2, soon)
    copies[3].start()
    product(0, soon)
    for bits in (3, 1, 2, 0):
        product(bits, late)
    pass_on(soon)
    for copy in reduce_moves(late)[:4]:
        copy.start()
    finalize(soon)
    pass_on(late)
    factor = post_factor(soon)
    take2(0, soon, factor)
    forward_rows(soon)
    moves2(soon)[2].wait_recv()
    take2(1, soon, factor)
    moves2(soon)[3].wait_recv()
    take2(2, soon, factor)
    finalize(late)
    moves2(soon)[4].wait_recv()
    moves2(soon)[5].wait_recv()
    take2(3, soon, factor)
    finish2(soon)

    @pl.when(next_row)
    def _():
        tail.start()

    @pl.when(s == 0)
    def _():
        kv2[:, :, 0:WINDOW, :] = jnp.zeros((2, kv_heads, WINDOW, HEAD_DIM), BF16)

    factor = post_factor(late)
    take2(0, late, factor)
    forward_rows(late)
    moves2(late)[2].wait_recv()
    take2(1, late, factor)
    moves2(late)[3].wait_recv()
    take2(2, late, factor)
    moves2(late)[4].wait_recv()
    moves2(late)[5].wait_recv()
    take2(3, late, factor)
    finish2(late)

    @pl.when(prev_row)
    def _():
        tail.wait_recv()

    for h in range(kv_heads):
        for part in range(2):
            q = q_all[h * group : (h + 1) * group, part * block : (part + 1) * block]
            q = q.reshape(group * block, HEAD_DIM)
            keys = kv2[0, h, part * block : part * block + WINDOW + block]
            values = kv2[1, h, part * block : part * block + WINDOW + block]
            scores = lax.dot_general(
                q, keys, (((1,), (1,)), ((), ())), preferred_element_type=F32
            )
            weights = jnp.exp2(jnp.tanh(scores * INNER) * OUTER)
            row = lax.broadcasted_iota(jnp.int32, (block, WINDOW + block), 0)
            col = lax.broadcasted_iota(jnp.int32, (block, WINDOW + block), 1)
            least = row
            if part == 0:
                least = jnp.maximum(row, jnp.where(prev_row, 0, WINDOW - 1))
            mask = (col > least) & (col <= row + WINDOW)
            weights = jnp.concatenate(
                [jnp.where(mask, weights[g * block : (g + 1) * block], 0.0) for g in range(group)],
                axis=0,
            )
            denominator = jnp.sum(weights, axis=-1, keepdims=True)
            numerator = jnp.dot(weights.astype(BF16), values, preferred_element_type=F32)
            result = (numerator / denominator).astype(BF16)
            for g in range(group):
                head = h * group + g
                o_ref[part * block : (part + 1) * block, head * HEAD_DIM : (head + 1) * HEAD_DIM] = (
                    result[g * block : (g + 1) * block]
                )

    def drain_first(part, carry):
        for copy in moves(part):
            copy.wait_send()

        @pl.when(has_up)
        def _():
            up(s, part).wait_send()

        @pl.when(c == 0)
        def _():
            side(s, part).wait_send()

        def drain_level(k, carry):
            @pl.when(has_up)
            def _():
                up(s - 2 * k, part).wait_send()

            side(s - 2 * k, part).wait_send()
            return carry

        lax.fori_loop(1, z + 1, drain_level, 0)
        return carry

    lax.fori_loop(0, PARTS, drain_first, 0)
    for part in range(2):
        for copy in (*reduce_moves(part), *swaps(part), *moves2(part)):
            copy.wait_send()

    @pl.when(next_row)
    def _():
        tail.wait_send()


def fused(x, gains, cos, sin, first, wo, second, count, collective_id):
    rows, cols = x.shape
    wq, wk, wv = first
    heads, kv_heads = wq.shape[1] // HEAD_DIM, wk.shape[1] // HEAD_DIM
    total = wq.shape[1] + 2 * wk.shape[1]
    depth = wo.shape[0]
    chunk, block = rows // PARTS, rows // 2
    vmem = pl.BlockSpec(memory_space=VMEM)
    hbm = pl.BlockSpec(memory_space=pltpu.HBM)
    dma = pltpu.SemaphoreType.DMA
    folded = [gain.reshape(-1, HEAD_DIM) for gain in gains]
    return pl.pallas_call(
        functools.partial(fused_kernel, count // 2, heads, kv_heads),
        out_shape=(
            jax.ShapeDtypeStruct((rows, cols), BF16),
            jax.ShapeDtypeStruct((rows, heads * HEAD_DIM), BF16),
        ),
        in_specs=[hbm] * 4 + [vmem] * 2 + [hbm] * 7,
        out_specs=(vmem, vmem),
        scratch_shapes=[
            VMEM((4, rows, cols), BF16),
            VMEM((4, cols, total), BF16),
            VMEM((4, depth, cols), BF16),
            VMEM((3,) + folded[0].shape, F32),
            VMEM((block, cols), BF16),
            VMEM((block, total), F32),
            VMEM((block, HEAD_DIM), F32),
            VMEM((heads, rows, HEAD_DIM), BF16),
            VMEM((count, 2, kv_heads, rows, HEAD_DIM), BF16),
            VMEM((heads, rows, HEAD_DIM), F32),
            VMEM((heads, rows, HEAD_DIM), F32),
            VMEM((rows, depth), BF16),
            VMEM((3, rows, cols), BF16),
            VMEM((rows, cols), F32),
            VMEM((2, 6, block // 2, cols), BF16),
            VMEM((2, 2, block // 2, cols), BF16),
            VMEM((4, rows, cols), BF16),
            VMEM((2, 8, block), F32),
            VMEM((2, 3, 8, block), F32),
            VMEM((2, kv_heads, WINDOW + rows, HEAD_DIM), BF16),
            dma((PARTS,)),
            dma((3,)),
            dma((4, 3)),
            dma((4,)),
            dma((6 * PARTS + 12,)),
            dma((6 * PARTS + 12,)),
            dma((count * PARTS,)),
            dma((count * PARTS,)),
            dma((count * PARTS,)),
            dma((12,)),
            dma((12,)),
            dma((6,)),
            dma((6,)),
            dma((2,)),
        ],
        compiler_params=pltpu.CompilerParams(
            collective_id=collective_id, has_side_effects=True, vmem_limit_bytes=58 * 2**20
        ),
        name="fused",
    )(x, *folded, cos, sin, wq, wk, wv, wo, *second)


def rms_scaled(values, weights):
    widened = values.astype(F32)
    factor = lax.rsqrt(jnp.mean(widened * widened, axis=-1, keepdims=True) + NORM_EPS)
    return widened * factor * weights


def plain_gather_project(x, gain, cos, sin, wq, wk, wv):
    full = lax.all_gather(x, "tp", axis=1, tiled=True)
    normed = rms_scaled(full, gain).astype(BF16)

    def heads_of(weight):
        product = jnp.dot(normed, weight, preferred_element_type=F32)
        return jnp.swapaxes(product.reshape(x.shape[0], -1, HEAD_DIM), 0, 1)

    def rotated(u):
        return (u * cos + jnp.roll(u, HEAD_DIM // 2, axis=-1) * sin).astype(BF16)

    keys, values = rotated(heads_of(wk)), heads_of(wv).astype(BF16)
    return rotated(heads_of(wq)), jnp.stack([keys, values])


def plain_output_project(attended, tokens, gain, wo):
    cols = tokens.shape[1]
    partial_sum = jnp.dot(attended, wo, preferred_element_type=F32).astype(BF16)
    summed = lax.psum(partial_sum, "tp").astype(F32)
    added = rms_scaled(summed, gain)
    mine = lax.dynamic_slice_in_dim(added, lax.axis_index("tp") * cols, cols, 1)
    return (tokens.astype(F32) + mine).astype(BF16)


def local(
    sizes,
    tokens,
    attention_gain,
    query_weight,
    key_weight,
    value_weight,
    output_weight,
    post_gain,
    local_gain,
    local_query_weight,
    local_key_weight,
    local_value_weight,
):
    seq, tp = sizes
    rows, cols = tokens.shape
    places = lax.axis_index("seq") * rows + lax.iota(jnp.int32, rows)
    halfway = HEAD_DIM // 2
    exponents = jnp.arange(halfway, dtype=F32) * (2.0 / HEAD_DIM)
    frequency = jnp.power(F32(10000.0), -exponents)
    angles = places.astype(F32)[:, None] * frequency[None, :]
    cosine, sine = jnp.cos(angles), jnp.sin(angles)
    cos = jnp.concatenate([cosine, cosine], axis=-1)
    sin = jnp.concatenate([-sine, sine], axis=-1)
    first = (query_weight, key_weight, value_weight)
    second = (local_query_weight, local_key_weight, local_value_weight)
    if tp == 4 and cols % HEAD_DIM == 0 and rows == 2 * WINDOW and seq % 2 == 0:
        gains = (attention_gain, post_gain, local_gain)
        return fused(tokens, gains, cos, sin, first, output_weight, second, seq, 0)
    lead = plain_gather_project(tokens, attention_gain, cos, sin, *first)
    attended = causal_attention(*lead, seq, 1)
    hidden = plain_output_project(attended, tokens, post_gain, output_weight)
    lq, lkv = plain_gather_project(hidden, local_gain, cos, sin, *second)
    return hidden, window_attention(lq, lkv, seq, 4)


def solution(mesh):
    in_specs = (
        P("seq", "tp"),
        P(),
        P(None, "tp"),
        P(None, "tp"),
        P(None, "tp"),
        P("tp", None),
        P(),
        P(),
        P(None, "tp"),
        P(None, "tp"),
        P(None, "tp"),
    )
    out_specs = (P("seq", "tp"), P("seq", "tp"))
    sizes = (mesh.shape["seq"], mesh.shape["tp"])
    body = functools.partial(local, sizes)
    return jax.shard_map(body, mesh=mesh, in_specs=in_specs, out_specs=out_specs, check_vma=False)
```

time: 131 us -> 105 us (0.80)
  Pallas kernels: 123 us -> 99.1 us
  local copies, waits for them, and re-layouts: 6.18 us -> 3.79 us
    pallas_call x4 -> x1, Pallas kernels: 123 us -> 99.1 us  [fused(): pl.pallas_call(functools.partial(fused_kernel, count // 2, heads, kv_head...]
    unnamed x18 -> x2, local copies, waits for them, and re-layouts: 5.26 us -> 3.79 us
where the time goes in v1:
time: 105 us
  Pallas kernels  99.1 us (94%)
  local copies, waits for them, and re-layouts  3.79 us (4%)
  other arithmetic  1.39 us (1%)
    pallas_call x1, Pallas kernels, fused(): pl.pallas_call(functools.partial(fused_kernel, count // 2, heads, kv_head...  99.1 us
    unnamed x2, local copies, waits for them, and re-layouts  3.79 us

profile of v1, /device:TPU:24, one launch (start us, length us, event | category | flops | bytes accessed | tf_op | source)
XLA Modules:
  0.0 104.9 jit_solution(5496193202413304583)
XLA Ops:
  0.7 0.5 fusion
  1.2 0.8 pad_maximum_fusion
  2.0 99.1 %fused.1 = (bf16[256,1152]{1,0:T(8,128)(2,1)}, bf16[256,1024]{1,0:T(8,128)(2,1)}) custom-call(bf16[256,1152]{1,0:T(8,128)(2,1)} %x_hbm.1, f32[36,128]{1,0:T(8,128)} %bitcast.3, f32[36,128]{1,0:T(8,128)} %bitcast.4, f32[36,128]{1,0:T(8,128)} %bitcast.5, f32[256,128]{1,0:T(8,128)} %get-tuple-element.5.cos_ref, f32[256,128]{1,0:T(8,128)} %get-tuple-element.6.sin_ref, ...), custom_call_target="tpu_custom_call" | custom-call | tf_op jit(solution)/shard_map/fused/pallas_call | solution.py:851
  101.1 1.9 %copy.15 = bf16[256,1152]{1,0:T(8,128)(2,1)} copy(bf16[256,1152]{1,0:T(8,128)(2,1)} %get-tuple-element.9) | data formatting | bytes 1179648
  103.0 1.9 %copy.16 = bf16[256,1024]{1,0:T(8,128)(2,1)} copy(bf16[256,1024]{1,0:T(8,128)(2,1)} %get-tuple-element.10) | data formatting | bytes 1048576
  (2 shorter events, 0.0 us)

commit v2 on v1

--- a/solution.py
+++ b/solution.py
@@ -285,25 +285,28 @@
 
 
 def fused_kernel(
-    levels, heads, kv_heads,
+    levels, heads, kv_heads, keep,
     x_hbm, gain1_hbm, gain2_hbm, gain3_hbm, cos_ref, sin_ref,
     wq_hbm, wk_hbm, wv_hbm, wo_hbm, lwq_hbm, lwk_hbm, lwv_hbm,
-    hidden_ref, o_ref,
-    buf, w, wo, gains, xg, acc, ss, q_all, kv_buf, out, lsum, att,
-    terms, own, landed, passed, proj, mine, stats, kv2,
+    hidden_ref, lq_ref, kv2,
+    buf, w, wo, gains, xg, acc, ss, ss_first, q_all, kv_buf, out, lsum, att,
+    terms, own, landed, passed, proj, mine, stats, q_up, out_up, lsum_up, up_num, up_sum, got_num, got_sum,
     x_sem, gain_sem, w_sem, wo_sem, ag_send, ag_recv, up_sem, side_sem, kv_sem,
-    rs_send, rs_recv, st_send, st_recv, tail_sem,
+    rs_send, rs_recv, st_send, st_recv, tail_sem, down_send, down_recv, back_send, back_recv,
 ):
     me = lax.axis_index("tp")
     s = lax.axis_index("seq")
     z, c = s // 2, s % 2
     mate = s + 1 - 2 * c
     has_up, has_down = z < levels - 1, z > 0
+    top, helper = z == levels - 1, z == levels - 2
     next_row, prev_row = s < 2 * levels - 1, s > 0
     rows, cols = hidden_ref.shape
     chunk_rows, half_rows = rows // PARTS, rows // PARTS // 2
     block, half = rows // 2, rows // 4
     chunks = cols // HEAD_DIM
+    ones = jnp.ones((8, HEAD_DIM), F32)
+    highest = lax.Precision.HIGHEST
     owners = [xor(me, bits) for bits in range(4)]
     peers = [{"tp": owner} for owner in owners]
     along_x, along_y = peers[1], peers[2]
@@ -339,15 +342,10 @@
         return loads
 
     first_loads = weight_loads(wk_hbm, wv_hbm, wq_hbm)
-    for bundle in first_loads:
-        for copy in bundle:
-            copy.start()
     wo_loads = []
     for bits in (3, 1, 2, 0):
         span = pl.ds(pl.multiple_of(owners[bits] * cols, cols), cols)
-        copy = pltpu.make_async_copy(wo_hbm.at[:, span], wo.at[bits], wo_sem.at[bits])
-        copy.start()
-        wo_loads.append(copy)
+        wo_loads.append(pltpu.make_async_copy(wo_hbm.at[:, span], wo.at[bits], wo_sem.at[bits]))
 
     barrier = pltpu.get_barrier_semaphore()
     for peer in (*peers[1:], {"seq": mate}):
@@ -398,25 +396,55 @@
     def moves2(part):
         return gather_moves(proj, 6 * PARTS, block, part, 0)
 
-    def kv_part(owner, part):
-        return kv_buf.at[owner, :, :, pl.ds(pl.multiple_of(part * chunk_rows, chunk_rows), chunk_rows)]
-
-    def up(owner, part):
-        at, ref = owner * PARTS + part, kv_part(owner, part)
+    def kv_part(owner, part, count):
+        here = pl.ds(pl.multiple_of(part * chunk_rows, chunk_rows), chunk_rows)
+        return kv_buf.at[owner, :, pl.ds(0, count), here]
+
+    def up(owner, part, count):
+        at, ref = owner * PARTS + part, kv_part(owner, part, count)
         return remote(ref, ref, up_sem.at[at], kv_sem.at[at], {"seq": s + 2})
 
-    def side(owner, part):
-        at, ref = owner * PARTS + part, kv_part(owner, part)
+    def side(owner, part, count):
+        at, ref = owner * PARTS + part, kv_part(owner, part, count)
         return remote(ref, ref, side_sem.at[at], kv_sem.at[at], {"seq": mate})
 
+    def lift(owner, part, act):
+        @pl.when(z < levels - 2)
+        def _():
+            act(up(owner, part, kv_heads))
+
+        @pl.when(helper)
+        def _():
+            act(up(owner, part, keep))
+
+    def launch(copy):
+        copy.start()
+
+    def sent(copy):
+        copy.wait_send()
+
     def arrive(owner, part):
-        up(owner, part).wait_recv()
-
-        @pl.when(has_up)
-        def _():
-            up(owner, part).start()
-
-        side(owner, part).start()
+        up(owner, part, kv_heads).wait_recv()
+        side(owner, part, kv_heads).start()
+        lift(owner, part, launch)
+
+    def arrive_top(owner, part):
+        up(owner, part, keep).wait_recv()
+        side(owner, part, keep).start()
+
+    down_heads = pl.ds(keep * group, group)
+
+    def query_down(part):
+        span = pl.ds(pl.multiple_of(part * block, block), block)
+        return remote(
+            q_all.at[down_heads, span], q_up.at[:, span], down_send.at[part], down_recv.at[part],
+            {"seq": s - 2},
+        )
+
+    backs = [
+        remote(source, target, back_send.at[i], back_recv.at[i], {"seq": s + 2})
+        for i, (source, target) in enumerate(((up_sum, got_sum), (up_num, got_num)))
+    ]
 
     def multiply(slot, count, begin, width, fresh):
         product = jnp.dot(
@@ -437,15 +465,15 @@
             lanes = slice(j * HEAD_DIM, (j + 1) * HEAD_DIM)
             wide = buf[slot, here, lanes].astype(F32)
             squares = wide * wide if squares is None else squares + wide * wide
-            xg[0:chunk_rows, lanes] = (wide * gain_row(0, slot, j)).astype(BF16)
+            proj[slot, here, lanes] = (wide * gain_row(0, slot, j)).astype(BF16)
         if slot == 0:
-            ss[0:chunk_rows, :] = squares
+            ss_first[here, :] = squares
         else:
-            ss[0:chunk_rows, :] += squares
-
-    def row_factor(count):
-        total = jnp.sum(ss[0:count, :], axis=-1, keepdims=True)
-        return lax.rsqrt(jnp.broadcast_to(total, (count, HEAD_DIM)) * (1.0 / D) + NORM_EPS)
+            ss_first[here, :] += squares
+
+    def row_factor(squares):
+        total = jnp.sum(squares, axis=-1, keepdims=True)
+        return lax.rsqrt(jnp.broadcast_to(total, squares.shape) * (1.0 / D) + NORM_EPS)
 
     def rotated(begin, count, factor, span):
         u = acc[0:count, begin : begin + HEAD_DIM] * factor
@@ -454,43 +482,86 @@
 
     for copy in x_loads[:1]:
         copy.wait()
-    for copy in moves(0)[:4]:
-        copy.start()
+    def launch_group(part, some):
+        copies = moves(part)
+        for i in some:
+            copies[i].start()
+
+    launch_group(0, range(4))
     for copy in x_loads[1:]:
         copy.wait()
+    launch_group(1, range(2))
     for copy in gain_loads:
         copy.wait()
+    for bundle in first_loads:
+        for copy in bundle[:2]:
+            copy.start()
 
     def first_part(part, carry):
+        with jax.named_scope("first_part"):
+            return one_part(part, carry)
+
+    def relay(part):
+        copies = moves(part)
+        copies[0].wait_recv()
+        copies[4].start()
+        copies[1].wait_recv()
+        copies[5].start()
+
+        @pl.when(part < PARTS - 1)
+        def _():
+            launch_group(part + 1, (2, 3))
+
+        @pl.when(part < PARTS - 2)
+        def _():
+            launch_group(part + 2, (0, 1))
+
+    def one_part(part, carry):
+        span = pl.ds(pl.multiple_of(part * chunk_rows, chunk_rows), chunk_rows)
+
         def take(slot):
             prepare(slot, part)
 
             @pl.when(part == 0)
             def _():
-                for copy in first_loads[slot]:
+                for copy in first_loads[slot][:2]:
                     copy.wait()
 
-            multiply(slot, chunk_rows, 0, kvc, slot == 0)
-
-        sends = moves(part)
+            product = jnp.dot(proj[slot, span, :], w[slot, :, 0:kvc], preferred_element_type=F32)
+            if slot == 0:
+                acc[0:chunk_rows, 0:kvc] = product
+            else:
+                acc[0:chunk_rows, 0:kvc] += product
+
+        copies = moves(part)
         take(0)
-        multiply(0, chunk_rows, kvc, qc, True)
-        sends[0].wait_recv()
-        sends[4].start()
-        sends[1].wait_recv()
-        sends[5].start()
+
+        @pl.when(part == 0)
+        def _():
+            relay(0)
+
+        @pl.when(part == PARTS // 4)
+        def _():
+            for bundle in first_loads:
+                bundle[2].start()
+
+        @pl.when(part == PARTS // 2)
+        def _():
+            for copy in wo_loads:
+                copy.start()
+
+        copies[2].wait_recv()
+        take(1)
+        copies[3].wait_recv()
+        take(2)
 
         @pl.when(part < PARTS - 1)
         def _():
-            for copy in moves(part + 1)[:4]:
-                copy.start()
-
-        sends[2].wait_recv()
-        take(1)
-        multiply(1, chunk_rows, kvc, qc, False)
-        sends[3].wait_recv()
-        take(2)
-        multiply(2, chunk_rows, kvc, qc, False)
+            relay(part + 1)
+
+        @pl.when(part == PARTS // 2)
+        def _():
+            queries(0)
 
         def forward(k, carry):
             @pl.when(part >= k)
@@ -503,11 +574,10 @@
         def _():
             lax.fori_loop(1, z + 1, forward, 0)
 
-        sends[4].wait_recv()
-        sends[5].wait_recv()
+        copies[4].wait_recv()
+        copies[5].wait_recv()
         take(3)
-        span = pl.ds(pl.multiple_of(part * chunk_rows, chunk_rows), chunk_rows)
-        factor = row_factor(chunk_rows)
+        factor = row_factor(ss_first[span, :])
         for h in range(kv_heads):
             kv_buf[s, 0, h, span, :] = rotated(h * HEAD_DIM, chunk_rows, factor, span)
             place = kc + h * HEAD_DIM
@@ -515,43 +585,95 @@
                 acc[0:chunk_rows, place : place + HEAD_DIM] * factor
             ).astype(BF16)
 
-        @pl.when(has_up)
-        def _():
-            up(s, part).start()
-
-        @pl.when(c == 0)
-        def _():
-            side(s, part).start()
-
-        multiply(3, chunk_rows, kvc, qc, False)
-        for h in range(heads):
-            q_all[h, span, :] = rotated(kvc + h * HEAD_DIM, chunk_rows, factor, span)
+        @pl.when((c == 0) | helper)
+        def _():
+            side(s, part, kv_heads).start()
+
+        lift(s, part, launch)
         return carry
 
+    def queries(which):
+        span = pl.ds(pl.multiple_of(which * block, block), block)
+
+        if which == 0:
+            for bundle in first_loads:
+                bundle[2].wait()
+
+        acc[:, kvc : kvc + qc] = sum(
+            jnp.dot(proj[slot, span, :], w[slot, :, kvc : kvc + qc], preferred_element_type=F32)
+            for slot in range(4)
+        )
+        factor = row_factor(ss_first[span, :])
+        for h in reversed(range(heads)):
+            q_all[h, span, :] = rotated(kvc + h * HEAD_DIM, block, factor, span)
+
+        @pl.when(top)
+        def _():
+            query_down(which).start()
+
     lax.fori_loop(0, PARTS, first_part, 0)
+    queries(1)
 
     second_loads = weight_loads(lwk_hbm, lwv_hbm, lwq_hbm)
-    for bundle in second_loads:
-        for copy in bundle:
+
+    def fetch(slot):
+        for copy in second_loads[slot]:
             copy.start()
 
-    for h in range(kv_heads):
-        attend(
-            q_all, kv_buf[s, 0, h], kv_buf[s, 1, h], out, lsum, h, group,
-            lambda row, col: col <= row, True,
-        )
-
-    def visit(owner):
+    with jax.named_scope("own"):
         for h in range(kv_heads):
+            attend(
+                q_all, kv_buf[s, 0, h], kv_buf[s, 1, h], out, lsum, h, group,
+                lambda row, col: col <= row, True,
+            )
+
+    def visit_heads(owner, begin, end):
+        for h in range(begin, end):
             attend(
                 q_all, kv_buf[owner, 0, h], kv_buf[owner, 1, h], out, lsum, h, group, None, False
             )
 
+    def visit(owner):
+        with jax.named_scope("visit"):
+            visit_heads(owner, 0, keep)
+
+            @pl.when(z < levels - 1)
+            def _():
+                visit_heads(owner, keep, kv_heads)
+
+    def visit_up(owner, first):
+        with jax.named_scope("visit_up"):
+            attend(
+                q_up, kv_buf[owner, 0, keep], kv_buf[owner, 1, keep], out_up, lsum_up, 0, group,
+                None, first,
+            )
+
+    def send_back():
+        for g in range(group):
+            up_sum[g] = lax.dot_general(
+                ones, lsum_up[g], (((1,), (1,)), ((), ())), precision=highest,
+                preferred_element_type=F32,
+            )
+            up_num[g] = out_up[g].astype(BF16)
+        for copy in backs:
+            copy.start()
+
+    @pl.when(helper | (c == 1))
+    def _():
+        for part in range(PARTS):
+            side(mate, part, kv_heads).wait_recv()
+
     @pl.when(c == 1)
     def _():
-        for part in range(PARTS):
-            side(s - 1, part).wait_recv()
-        visit(s - 1)
+        with jax.named_scope("mate"):
+            visit_heads(s - 1, 0, kv_heads)
+
+    @pl.when(helper)
+    def _():
+        for part in range(2):
+            query_down(part).wait_recv()
+        visit_up(s, True)
+        visit_up(mate, False)
 
     def turn(r, carry):
         def level(k, carry):
@@ -561,17 +683,37 @@
             def _():
                 owner, other = s - 2 * k, mate - 2 * k
 
-                @pl.when((r >= PARTS) | (z == levels - 1))
+                @pl.when(top)
+                def _():
+                    arrive_top(owner, part)
+
+                @pl.when((r >= PARTS) & has_up)
                 def _():
                     arrive(owner, part)
 
                 @pl.when(part == PARTS - 1)
                 def _():
+                    @pl.when(helper)
+                    def _():
+                        visit_up(owner, False)
+                        for p in range(PARTS):
+                            side(other, p, kv_heads).wait_recv()
+                        visit_up(other, False)
+
+                        @pl.when(k == z)
+                        def _():
+                            send_back()
+
                     def both(j, carry):
-                        @pl.when(j == 1)
+                        @pl.when((j == 1) & top)
                         def _():
                             for p in range(PARTS):
-                                side(other, p).wait_recv()
+                                side(other, p, keep).wait_recv()
+
+                        @pl.when((j == 1) & (z < levels - 2))
+                        def _():
+                            for p in range(PARTS):
+                                side(other, p, kv_heads).wait_recv()
 
                         visit(owner + j * (other - owner))
                         return carry
@@ -584,7 +726,21 @@
         return carry
 
     lax.fori_loop(1, PARTS + z, turn, 0)
-    write_heads(att, out, lsum)
+
+    @pl.when(top)
+    def _():
+        for copy in backs:
+            copy.wait_recv()
+        for g in range(group):
+            column = lax.dot_general(
+                got_sum[g], ones * (0.125 / HEAD_DIM), (((0,), (0,)), ((), ())), precision=highest,
+                preferred_element_type=F32,
+            )
+            lsum[keep * group + g] += column
+            out[keep * group + g] += got_num[g].astype(F32)
+
+    with jax.named_scope("write_heads"):
+        write_heads(att, out, lsum)
 
     def reduce_moves(part):
         base = part * block
@@ -625,9 +781,6 @@
             terms[0, base + half : base + block].astype(F32) + landed[part, 1].astype(F32)
         ).astype(BF16)
         copies[4].start()
-
-    ones = jnp.ones((8, HEAD_DIM), F32)
-    highest = lax.Precision.HIGHEST
 
     def swaps(part):
         return [
@@ -706,50 +859,58 @@
     def finish2(part):
         span = pl.ds(part * block, block)
         place_rows = pl.ds(WINDOW + part * block, block)
-        factor = row_factor(block)
+        factor = row_factor(ss[...])
         for h in range(kv_heads):
             kv2[0, h, place_rows, :] = rotated(h * HEAD_DIM, block, factor, span)
             place = kc + h * HEAD_DIM
             kv2[1, h, place_rows, :] = (acc[:, place : place + HEAD_DIM] * factor).astype(BF16)
         for h in range(heads):
-            q_all[h, span, :] = rotated(kvc + h * HEAD_DIM, block, factor, span)
+            lq_ref[h, span, :] = rotated(kvc + h * HEAD_DIM, block, factor, span)
 
     tail = remote(
         kv2.at[:, :, pl.ds(rows, WINDOW)], kv2.at[:, :, pl.ds(0, WINDOW)],
         tail_sem.at[0], tail_sem.at[1], {"seq": s + 1},
     )
 
+    def scoped(name, run, *given):
+        with jax.named_scope(name):
+            return run(*given)
+
     for copy in wo_loads:
         copy.wait()
     late, soon = 0, 1
     copies = reduce_moves(soon)
-    product(3, soon)
+    scoped("product", product, 3, soon)
     copies[0].start()
     copies[1].start()
-    product(1, soon)
+    scoped("product", product, 1, soon)
     copies[2].start()
-    product(2, soon)
+    scoped("product", product, 2, soon)
     copies[3].start()
-    product(0, soon)
+    scoped("product", product, 0, soon)
+    fetch(0)
     for bits in (3, 1, 2, 0):
-        product(bits, late)
-    pass_on(soon)
+        scoped("product", product, bits, late)
+    scoped("pass_on", pass_on, soon)
     for copy in reduce_moves(late)[:4]:
         copy.start()
-    finalize(soon)
-    pass_on(late)
-    factor = post_factor(soon)
-    take2(0, soon, factor)
-    forward_rows(soon)
+    fetch(1)
+    fetch(2)
+    fetch(3)
+    scoped("finalize", finalize, soon)
+    scoped("pass_on", pass_on, late)
+    factor = scoped("post_factor", post_factor, soon)
+    scoped("take2", take2, 0, soon, factor)
+    scoped("forward_rows", forward_rows, soon)
     moves2(soon)[2].wait_recv()
-    take2(1, soon, factor)
+    scoped("take2", take2, 1, soon, factor)
     moves2(soon)[3].wait_recv()
-    take2(2, soon, factor)
-    finalize(late)
+    scoped("take2", take2, 2, soon, factor)
+    scoped("finalize", finalize, late)
     moves2(soon)[4].wait_recv()
     moves2(soon)[5].wait_recv()
-    take2(3, soon, factor)
-    finish2(soon)
+    scoped("take2", take2, 3, soon, factor)
+    scoped("finish2", finish2, soon)
 
     @pl.when(next_row)
     def _():
@@ -759,75 +920,60 @@
     def _():
         kv2[:, :, 0:WINDOW, :] = jnp.zeros((2, kv_heads, WINDOW, HEAD_DIM), BF16)
 
-    factor = post_factor(late)
-    take2(0, late, factor)
-    forward_rows(late)
+    factor = scoped("post_factor", post_factor, late)
+    scoped("take2", take2, 0, late, factor)
+    scoped("forward_rows", forward_rows, late)
     moves2(late)[2].wait_recv()
-    take2(1, late, factor)
+    scoped("take2", take2, 1, late, factor)
     moves2(late)[3].wait_recv()
-    take2(2, late, factor)
+    scoped("take2", take2, 2, late, factor)
     moves2(late)[4].wait_recv()
     moves2(late)[5].wait_recv()
-    take2(3, late, factor)
-    finish2(late)
+    scoped("take2", take2, 3, late, factor)
+    scoped("finish2", finish2, late)
 
     @pl.when(prev_row)
     def _():
         tail.wait_recv()
-
-    for h in range(kv_heads):
-        for part in range(2):
-            q = q_all[h * group : (h + 1) * group, part * block : (part + 1) * block]
-            q = q.reshape(group * block, HEAD_DIM)
-            keys = kv2[0, h, part * block : part * block + WINDOW + block]
-            values = kv2[1, h, part * block : part * block + WINDOW + block]
-            scores = lax.dot_general(
-                q, keys, (((1,), (1,)), ((), ())), preferred_element_type=F32
-            )
-            weights = jnp.exp2(jnp.tanh(scores * INNER) * OUTER)
-            row = lax.broadcasted_iota(jnp.int32, (block, WINDOW + block), 0)
-            col = lax.broadcasted_iota(jnp.int32, (block, WINDOW + block), 1)
-            least = row
-            if part == 0:
-                least = jnp.maximum(row, jnp.where(prev_row, 0, WINDOW - 1))
-            mask = (col > least) & (col <= row + WINDOW)
-            weights = jnp.concatenate(
-                [jnp.where(mask, weights[g * block : (g + 1) * block], 0.0) for g in range(group)],
-                axis=0,
-            )
-            denominator = jnp.sum(weights, axis=-1, keepdims=True)
-            numerator = jnp.dot(weights.astype(BF16), values, preferred_element_type=F32)
-            result = (numerator / denominator).astype(BF16)
-            for g in range(group):
-                head = h * group + g
-                o_ref[part * block : (part + 1) * block, head * HEAD_DIM : (head + 1) * HEAD_DIM] = (
-                    result[g * block : (g + 1) * block]
-                )
 
     def drain_first(part, carry):
         for copy in moves(part):
             copy.wait_send()
 
-        @pl.when(has_up)
-        def _():
-            up(s, part).wait_send()
-
-        @pl.when(c == 0)
-        def _():
-            side(s, part).wait_send()
+        lift(s, part, sent)
+
+        @pl.when((c == 0) | helper)
+        def _():
+            side(s, part, kv_heads).wait_send()
 
         def drain_level(k, carry):
+            lift(s - 2 * k, part, sent)
+
             @pl.when(has_up)
             def _():
-                up(s - 2 * k, part).wait_send()
-
-            side(s - 2 * k, part).wait_send()
+                side(s - 2 * k, part, kv_heads).wait_send()
+
+            @pl.when(top)
+            def _():
+                side(s - 2 * k, part, keep).wait_send()
+
             return carry
 
         lax.fori_loop(1, z + 1, drain_level, 0)
         return carry
 
     lax.fori_loop(0, PARTS, drain_first, 0)
+
+    @pl.when(helper)
+    def _():
+        for copy in backs:
+            copy.wait_send()
+
+    @pl.when(top)
+    def _():
+        for part in range(2):
+            query_down(part).wait_send()
+
     for part in range(2):
         for copy in (*reduce_moves(part), *swaps(part), *moves2(part)):
             copy.wait_send()
@@ -843,19 +989,22 @@
     heads, kv_heads = wq.shape[1] // HEAD_DIM, wk.shape[1] // HEAD_DIM
     total = wq.shape[1] + 2 * wk.shape[1]
     depth = wo.shape[0]
-    chunk, block = rows // PARTS, rows // 2
+    group, block = heads // kv_heads, rows // 2
     vmem = pl.BlockSpec(memory_space=VMEM)
     hbm = pl.BlockSpec(memory_space=pltpu.HBM)
     dma = pltpu.SemaphoreType.DMA
     folded = [gain.reshape(-1, HEAD_DIM) for gain in gains]
+    far = [x, *folded, wq, wk, wv, wo, *second]
+    far = [pltpu.with_memory_space_constraint(array, pltpu.HBM) for array in far]
     return pl.pallas_call(
-        functools.partial(fused_kernel, count // 2, heads, kv_heads),
+        functools.partial(fused_kernel, count // 2, heads, kv_heads, kv_heads - 1),
         out_shape=(
             jax.ShapeDtypeStruct((rows, cols), BF16),
-            jax.ShapeDtypeStruct((rows, heads * HEAD_DIM), BF16),
+            jax.ShapeDtypeStruct((heads, rows, HEAD_DIM), BF16),
+            jax.ShapeDtypeStruct((2, kv_heads, WINDOW + rows, HEAD_DIM), BF16),
         ),
         in_specs=[hbm] * 4 + [vmem] * 2 + [hbm] * 7,
-        out_specs=(vmem, vmem),
+        out_specs=(vmem, vmem, vmem),
         scratch_shapes=[
             VMEM((4, rows, cols), BF16),
             VMEM((4, cols, total), BF16),
@@ -864,6 +1013,7 @@
             VMEM((block, cols), BF16),
             VMEM((block, total), F32),
             VMEM((block, HEAD_DIM), F32),
+            VMEM((rows, HEAD_DIM), F32),
             VMEM((heads, rows, HEAD_DIM), BF16),
             VMEM((count, 2, kv_heads, rows, HEAD_DIM), BF16),
             VMEM((heads, rows, HEAD_DIM), F32),
@@ -876,7 +1026,13 @@
             VMEM((4, rows, cols), BF16),
             VMEM((2, 8, block), F32),
             VMEM((2, 3, 8, block), F32),
-            VMEM((2, kv_heads, WINDOW + rows, HEAD_DIM), BF16),
+            VMEM((group, rows, HEAD_DIM), BF16),
+            VMEM((group, rows, HEAD_DIM), F32),
+            VMEM((group, rows, HEAD_DIM), F32),
+            VMEM((group, rows, HEAD_DIM), BF16),
+            VMEM((group, 8, rows), F32),
+            VMEM((group, rows, HEAD_DIM), BF16),
+            VMEM((group, 8, rows), F32),
             dma((PARTS,)),
             dma((3,)),
             dma((4, 3)),
@@ -891,12 +1047,76 @@
             dma((6,)),
             dma((6,)),
             dma((2,)),
+            dma((2,)),
+            dma((2,)),
+            dma((2,)),
+            dma((2,)),
         ],
         compiler_params=pltpu.CompilerParams(
-            collective_id=collective_id, has_side_effects=True, vmem_limit_bytes=58 * 2**20
+            collective_id=collective_id, has_side_effects=True, vmem_limit_bytes=50 * 2**20
         ),
         name="fused",
-    )(x, *folded, cos, sin, wq, wk, wv, wo, *second)
+    )(*far[:4], cos, sin, *far[4:])
+
+
+def finish_kernel(hid_ref, q_ref, kv_ref, hid_hbm, o_hbm, o_ref, sems):
+    rows = hid_ref.shape[0]
+    heads, kv_heads = q_ref.shape[0], kv_ref.shape[1]
+    group, block = heads // kv_heads, rows // 2
+    begins = jnp.where(lax.axis_index("seq") > 0, 0, WINDOW - 1)
+    copies = [pltpu.make_async_copy(hid_ref, hid_hbm, sems.at[kv_heads])]
+    copies[0].start()
+    for h in range(kv_heads):
+        for part in range(2):
+            q = q_ref[h * group : (h + 1) * group, part * block : (part + 1) * block]
+            q = q.reshape(group * block, HEAD_DIM)
+            keys = kv_ref[0, h, part * block : part * block + WINDOW + block]
+            values = kv_ref[1, h, part * block : part * block + WINDOW + block]
+            scores = lax.dot_general(
+                q, keys, (((1,), (1,)), ((), ())), preferred_element_type=F32
+            )
+            weights = jnp.exp2(jnp.tanh(scores * INNER) * OUTER)
+            row = lax.broadcasted_iota(jnp.int32, (block, WINDOW + block), 0)
+            col = lax.broadcasted_iota(jnp.int32, (block, WINDOW + block), 1)
+            least = jnp.maximum(row, begins) if part == 0 else row
+            mask = (col > least) & (col <= row + WINDOW)
+            weights = jnp.concatenate(
+                [jnp.where(mask, weights[g * block : (g + 1) * block], 0.0) for g in range(group)],
+                axis=0,
+            )
+            denominator = jnp.sum(weights, axis=-1, keepdims=True)
+            numerator = jnp.dot(weights.astype(BF16), values, preferred_element_type=F32)
+            result = (numerator / denominator).astype(BF16)
+            for g in range(group):
+                head = h * group + g
+                o_ref[part * block : (part + 1) * block, head * HEAD_DIM : (head + 1) * HEAD_DIM] = (
+                    result[g * block : (g + 1) * block]
+                )
+        lanes = pl.ds(h * group * HEAD_DIM, group * HEAD_DIM)
+        copy = pltpu.make_async_copy(o_ref.at[:, lanes], o_hbm.at[:, lanes], sems.at[h])
+        copy.start()
+        copies.append(copy)
+    for copy in copies:
+        copy.wait()
+
+
+def finish(hidden, q, kv):
+    heads, rows, _ = q.shape
+    vmem = pl.BlockSpec(memory_space=VMEM)
+    hbm = pl.BlockSpec(memory_space=pltpu.HBM)
+    shape = jax.ShapeDtypeStruct((rows, heads * HEAD_DIM), BF16)
+    return pl.pallas_call(
+        finish_kernel,
+        out_shape=(jax.ShapeDtypeStruct(hidden.shape, BF16), shape),
+        in_specs=[vmem] * 3,
+        out_specs=(hbm, hbm),
+        scratch_shapes=[
+            VMEM(shape.shape, BF16),
+            pltpu.SemaphoreType.DMA((kv.shape[1] + 1,)),
+        ],
+        compiler_params=pltpu.CompilerParams(vmem_limit_bytes=8 * 2**20),
+        name="finish",
+    )(hidden, q, kv)
 
 
 def rms_scaled(values, weights):
@@ -955,9 +1175,9 @@
     sin = jnp.concatenate([-sine, sine], axis=-1)
     first = (query_weight, key_weight, value_weight)
     second = (local_query_weight, local_key_weight, local_value_weight)
-    if tp == 4 and cols % HEAD_DIM == 0 and rows == 2 * WINDOW and seq % 2 == 0:
+    if tp == 4 and cols % HEAD_DIM == 0 and rows == 2 * WINDOW and seq % 2 == 0 and seq > 4:
         gains = (attention_gain, post_gain, local_gain)
-        return fused(tokens, gains, cos, sin, first, output_weight, second, seq, 0)
+        return finish(*fused(tokens, gains, cos, sin, first, output_weight, second, seq, 0))
     lead = plain_gather_project(tokens, attention_gain, cos, sin, *first)
     attended = causal_attention(*lead, seq, 1)
     hidden = plain_output_project(attended, tokens, post_gain, output_weight)

time: 105 us -> 94.8 us (0.903)
  Pallas kernels: 99.1 us -> 93.1 us
  local copies, waits for them, and re-layouts: 3.79 us -> 0 us
    pallas_call x1, Pallas kernels: 99.1 us -> 91.3 us  [fused(): pl.pallas_call(functools.partial(fused_kernel, count // 2, heads, kv_head...]
    unnamed x2 -> x0, local copies, waits for them, and re-layouts: 3.79 us -> none
    pallas_call x0 -> x1, Pallas kernels: none -> 1.79 us  [finish(): pl.pallas_call(finish_kernel, out_shape=(jax.ShapeDtypeStruct(hidden.shap...]
where the time goes in v2:
time: 94.8 us; the launch traced here: 94.6 us
  Pallas kernels  93.1 us (98%)
    pallas_call x1, Pallas kernels, fused(): pl.pallas_call(functools.partial(fused_kernel, count // 2, heads, kv_head...  91.3 us

profile of v2, /device:TPU:24, one launch (start us, length us, event | category | flops | bytes accessed | tf_op | source)
XLA Modules:
  0.0 94.6 jit_solution(2786951641724157118)
XLA Ops:
  0.7 0.5 fusion
  1.2 0.1 pad_maximum_fusion
  1.3 91.3 %fused.1 = (bf16[256,1152]{1,0:T(8,128)(2,1)S(1)}, bf16[8,256,128]{2,1,0:T(8,128)(2,1)S(1)}, bf16[2,4,384,128]{3,2,1,0:T(8,128)(2,1)S(1)}) custom-call(bf16[256,1152]{1,0:T(8,128)(2,1)} %x_hbm.1, f32[36,128]{1,0:T(8,128)} %bitcast.3, f32[36,128]{1,0:T(8,128)} %bitcast.4, f32[36,128]{1,0:T(8,128)} %bitcast.5, f32[256,128]{1,0:T(8,128)S(1)} %get-tuple-element.11.cos_ref, ...), custom_call_target="tpu_custom_call" | custom-call | tf_op jit(solution)/shard_map/fused/pallas_call | solution.py:999
  92.7 1.8 %finish.1 = (bf16[256,1152]{1,0:T(8,128)(2,1)}, bf16[256,1024]{1,0:T(8,128)(2,1)}) custom-call(bf16[256,1152]{1,0:T(8,128)(2,1)S(1)} %get-tuple-element.5.hid_ref, bf16[8,256,128]{2,1,0:T(8,128)(2,1)S(1)} %get-tuple-element.6.q_ref, bf16[2,4,384,128]{3,2,1,0:T(8,128)(2,1)S(1)} %get-tuple-element.7.kv_ref), custom_call_target="tpu_custom_call" | custom-call | tf_op jit(solution)/shard_map/finish/pallas_call | solution.py:1108
  (2 shorter events, 0.0 us)

commit v3 on v2

--- a/solution.py
+++ b/solution.py
@@ -3,6 +3,7 @@
 
 import jax
 import jax.numpy as jnp
+import numpy as np
 from jax import lax
 from jax.experimental import pallas as pl
 from jax.experimental.pallas import tpu as pltpu
@@ -286,11 +287,11 @@
 
 def fused_kernel(
     levels, heads, kv_heads, keep,
-    x_hbm, gain1_hbm, gain2_hbm, gain3_hbm, cos_ref, sin_ref,
+    x_hbm, gain1_hbm, gain2_hbm, gain3_hbm, fine_hbm, coarse_hbm,
     wq_hbm, wk_hbm, wv_hbm, wo_hbm, lwq_hbm, lwk_hbm, lwv_hbm,
     hidden_ref, lq_ref, kv2,
     buf, w, wo, gains, xg, acc, ss, ss_first, q_all, kv_buf, out, lsum, att,
-    terms, own, landed, passed, proj, mine, stats, q_up, out_up, lsum_up, up_num, up_sum, got_num, got_sum,
+    terms, own, landed, passed, proj, mine, stats, cos_ref, sin_ref, fine, coarse, q_up, out_up, lsum_up, up_num, up_sum, got_num, got_sum,
     x_sem, gain_sem, w_sem, wo_sem, ag_send, ag_recv, up_sem, side_sem, kv_sem,
     rs_send, rs_recv, st_send, st_recv, tail_sem, down_send, down_recv, back_send, back_recv,
 ):
@@ -321,8 +322,12 @@
         copy.start()
         x_loads.append(copy)
     gain_loads = []
-    for i, ref in enumerate((gain1_hbm, gain2_hbm, gain3_hbm)):
-        copy = pltpu.make_async_copy(ref, gains.at[i], gain_sem.at[i])
+    pairs = (
+        (gain1_hbm, gains.at[0]), (gain2_hbm, gains.at[1]), (gain3_hbm, gains.at[2]),
+        (fine_hbm, fine), (coarse_hbm, coarse),
+    )
+    for i, (ref, target) in enumerate(pairs):
+        copy = pltpu.make_async_copy(ref, target, gain_sem.at[i])
         copy.start()
         gain_loads.append(copy)
 
@@ -424,13 +429,15 @@
         copy.wait_send()
 
     def arrive(owner, part):
-        up(owner, part, kv_heads).wait_recv()
-        side(owner, part, kv_heads).start()
-        lift(owner, part, launch)
+        with jax.named_scope("arrive"):
+            up(owner, part, kv_heads).wait_recv()
+            side(owner, part, kv_heads).start()
+            lift(owner, part, launch)
 
     def arrive_top(owner, part):
-        up(owner, part, keep).wait_recv()
-        side(owner, part, keep).start()
+        with jax.named_scope("arrive_top"):
+            up(owner, part, keep).wait_recv()
+            side(owner, part, keep).start()
 
     down_heads = pl.ds(keep * group, group)
 
@@ -443,7 +450,13 @@
 
     backs = [
         remote(source, target, back_send.at[i], back_recv.at[i], {"seq": s + 2})
-        for i, (source, target) in enumerate(((up_sum, got_sum), (up_num, got_num)))
+        for i, (source, target) in enumerate(
+            (
+                (up_sum, got_sum),
+                (up_num.at[:, pl.ds(block, block)], got_num.at[:, pl.ds(block, block)]),
+                (up_num.at[:, pl.ds(0, block)], got_num.at[:, pl.ds(0, block)]),
+            )
+        )
     ]
 
     def multiply(slot, count, begin, width, fresh):
@@ -496,6 +509,11 @@
     for bundle in first_loads:
         for copy in bundle[:2]:
             copy.start()
+    for begin in range(0, rows, 64):
+        span = slice(begin, begin + 64)
+        cosine, sine = coarse[0, pl.ds(s, 1), :], coarse[1, pl.ds(s, 1), :]
+        cos_ref[span, :] = fine[0, span] * cosine - fine[1, span] * sine
+        sin_ref[span, :] = fine[1, span] * cosine + fine[0, span] * sine
 
     def first_part(part, carry):
         with jax.named_scope("first_part"):
@@ -562,17 +580,6 @@
         @pl.when(part == PARTS // 2)
         def _():
             queries(0)
-
-        def forward(k, carry):
-            @pl.when(part >= k)
-            def _():
-                arrive(s - 2 * k, part - k)
-
-            return carry
-
-        @pl.when(has_up)
-        def _():
-            lax.fori_loop(1, z + 1, forward, 0)
 
         copies[4].wait_recv()
         copies[5].wait_recv()
@@ -590,6 +597,18 @@
             side(s, part, kv_heads).start()
 
         lift(s, part, launch)
+
+        def forward(k, carry):
+            @pl.when(part >= 2 * k - 1)
+            def _():
+                arrive(s - 2 * k, part - 2 * k + 1)
+
+            return carry
+
+        @pl.when(has_up)
+        def _():
+            lax.fori_loop(1, z + 1, forward, 0)
+
         return carry
 
     def queries(which):
@@ -627,25 +646,28 @@
                 lambda row, col: col <= row, True,
             )
 
-    def visit_heads(owner, begin, end):
+    def visit_heads(owner, begin, end, span):
         for h in range(begin, end):
             attend(
-                q_all, kv_buf[owner, 0, h], kv_buf[owner, 1, h], out, lsum, h, group, None, False
+                q_all, kv_buf[owner, 0, h, span], kv_buf[owner, 1, h, span], out, lsum, h, group,
+                None, False,
             )
 
-    def visit(owner):
+    def visit(owner, span):
         with jax.named_scope("visit"):
-            visit_heads(owner, 0, keep)
-
-            @pl.when(z < levels - 1)
+            @pl.when(top)
             def _():
-                visit_heads(owner, keep, kv_heads)
-
-    def visit_up(owner, first):
+                visit_heads(owner, 0, keep, span)
+
+            @pl.when(has_up)
+            def _():
+                visit_heads(owner, 0, kv_heads, span)
+
+    def visit_up(owner, first, span):
         with jax.named_scope("visit_up"):
             attend(
-                q_up, kv_buf[owner, 0, keep], kv_buf[owner, 1, keep], out_up, lsum_up, 0, group,
-                None, first,
+                q_up, kv_buf[owner, 0, keep, span], kv_buf[owner, 1, keep, span], out_up, lsum_up,
+                0, group, None, first,
             )
 
     def send_back():
@@ -654,9 +676,13 @@
                 ones, lsum_up[g], (((1,), (1,)), ((), ())), precision=highest,
                 preferred_element_type=F32,
             )
-            up_num[g] = out_up[g].astype(BF16)
-        for copy in backs:
+        for part, copy in ((1, backs[1]), (0, backs[2])):
+            span = slice(part * block, (part + 1) * block)
+            for g in range(group):
+                up_num[g, span] = out_up[g, span].astype(BF16)
             copy.start()
+            if part == 1:
+                backs[0].start()
 
     @pl.when(helper | (c == 1))
     def _():
@@ -666,23 +692,21 @@
     @pl.when(c == 1)
     def _():
         with jax.named_scope("mate"):
-            visit_heads(s - 1, 0, kv_heads)
+            visit_heads(s - 1, 0, kv_heads, pl.ds(0, rows))
 
     @pl.when(helper)
     def _():
         for part in range(2):
             query_down(part).wait_recv()
-        visit_up(s, True)
-        visit_up(mate, False)
+        visit_up(s, True, pl.ds(0, rows))
+        visit_up(mate, False, pl.ds(0, rows))
 
     def turn(r, carry):
-        def level(k, carry):
-            part = r - k
+        def take_in(k, carry):
+            owner, part = s - 2 * k, r - 2 * k + 1
 
             @pl.when((part >= 0) & (part < PARTS))
             def _():
-                owner, other = s - 2 * k, mate - 2 * k
-
                 @pl.when(top)
                 def _():
                     arrive_top(owner, part)
@@ -691,56 +715,68 @@
                 def _():
                     arrive(owner, part)
 
-                @pl.when(part == PARTS - 1)
+            return carry
+
+        def level(k, carry):
+            owner, other = s - 2 * k, mate - 2 * k
+            whole = pl.ds(0, rows)
+
+            @pl.when(r - 2 * k + 1 == PARTS - 1)
+            def _():
+                @pl.when(helper)
                 def _():
-                    @pl.when(helper)
+                    visit_up(owner, False, whole)
+                    for p in range(PARTS):
+                        side(other, p, kv_heads).wait_recv()
+                    visit_up(other, False, whole)
+
+                    @pl.when(k == z)
                     def _():
-                        visit_up(owner, False)
+                        send_back()
+
+                def both(j, carry):
+                    @pl.when((j == 1) & top)
+                    def _():
+                        for p in range(PARTS):
+                            side(other, p, keep).wait_recv()
+
+                    @pl.when((j == 1) & (z < levels - 2))
+                    def _():
                         for p in range(PARTS):
                             side(other, p, kv_heads).wait_recv()
-                        visit_up(other, False)
-
-                        @pl.when(k == z)
-                        def _():
-                            send_back()
-
-                    def both(j, carry):
-                        @pl.when((j == 1) & top)
-                        def _():
-                            for p in range(PARTS):
-                                side(other, p, keep).wait_recv()
-
-                        @pl.when((j == 1) & (z < levels - 2))
-                        def _():
-                            for p in range(PARTS):
-                                side(other, p, kv_heads).wait_recv()
-
-                        visit(owner + j * (other - owner))
-                        return carry
-
-                    lax.fori_loop(0, 2, both, 0)
+
+                    visit(owner + j * (other - owner), whole)
+                    return carry
+
+                lax.fori_loop(0, 2, both, 0)
 
             return carry
 
+        lax.fori_loop(1, z + 1, take_in, 0)
         lax.fori_loop(1, z + 1, level, 0)
         return carry
 
-    lax.fori_loop(1, PARTS + z, turn, 0)
-
-    @pl.when(top)
-    def _():
-        for copy in backs:
-            copy.wait_recv()
-        for g in range(group):
-            column = lax.dot_general(
-                got_sum[g], ones * (0.125 / HEAD_DIM), (((0,), (0,)), ((), ())), precision=highest,
-                preferred_element_type=F32,
-            )
-            lsum[keep * group + g] += column
-            out[keep * group + g] += got_num[g].astype(F32)
-
-    with jax.named_scope("write_heads"):
-        write_heads(att, out, lsum)
+    lax.fori_loop(1, PARTS + 2 * z - 1, turn, 0)
+
+    def write_part(part):
+        span = slice(part * block, (part + 1) * block)
+
+        @pl.when(top)
+        def _():
+            if part == 1:
+                backs[0].wait_recv()
+            backs[2 - part].wait_recv()
+            for g in range(group):
+                column = lax.dot_general(
+                    got_sum[g, :, span], ones * (0.125 / HEAD_DIM), (((0,), (0,)), ((), ())),
+                    precision=highest, preferred_element_type=F32,
+                )
+                lsum[keep * group + g, span] += column
+                out[keep * group + g, span] += got_num[g, span].astype(F32)
+
+        for h in range(heads):
+            denominator = jnp.sum(lsum[h, span], axis=-1, keepdims=True)
+            att[span, h * HEAD_DIM : (h + 1) * HEAD_DIM] = (out[h, span] / denominator).astype(BF16)
 
     def reduce_moves(part):
         base = part * block
@@ -879,6 +915,7 @@
     for copy in wo_loads:
         copy.wait()
     late, soon = 0, 1
+    scoped("write_part", write_part, soon)
     copies = reduce_moves(soon)
     scoped("product", product, 3, soon)
     copies[0].start()
@@ -889,6 +926,7 @@
     copies[3].start()
     scoped("product", product, 0, soon)
     fetch(0)
+    scoped("write_part", write_part, late)
     for bits in (3, 1, 2, 0):
         scoped("product", product, bits, late)
     scoped("pass_on", pass_on, soon)
@@ -983,7 +1021,7 @@
         tail.wait_send()
 
 
-def fused(x, gains, cos, sin, first, wo, second, count, collective_id):
+def fused(x, gains, first, wo, second, count, collective_id):
     rows, cols = x.shape
     wq, wk, wv = first
     heads, kv_heads = wq.shape[1] // HEAD_DIM, wk.shape[1] // HEAD_DIM
@@ -994,7 +1032,16 @@
     hbm = pl.BlockSpec(memory_space=pltpu.HBM)
     dma = pltpu.SemaphoreType.DMA
     folded = [gain.reshape(-1, HEAD_DIM) for gain in gains]
-    far = [x, *folded, wq, wk, wv, wo, *second]
+    turns = 10000.0 ** (-2.0 * np.arange(HEAD_DIM // 2) / HEAD_DIM)
+    turns = np.concatenate([turns, turns])
+    sign = np.where(np.arange(HEAD_DIM) < HEAD_DIM // 2, -1.0, 1.0)
+
+    def table(places):
+        angles = places[:, None] * turns
+        return jnp.asarray(np.stack([np.cos(angles), sign * np.sin(angles)]), F32)
+
+    tables = (table(np.arange(rows)), table(np.arange(count) * rows))
+    far = [x, *folded, *tables, wq, wk, wv, wo, *second]
     far = [pltpu.with_memory_space_constraint(array, pltpu.HBM) for array in far]
     return pl.pallas_call(
         functools.partial(fused_kernel, count // 2, heads, kv_heads, kv_heads - 1),
@@ -1003,7 +1050,7 @@
             jax.ShapeDtypeStruct((heads, rows, HEAD_DIM), BF16),
             jax.ShapeDtypeStruct((2, kv_heads, WINDOW + rows, HEAD_DIM), BF16),
         ),
-        in_specs=[hbm] * 4 + [vmem] * 2 + [hbm] * 7,
+        in_specs=[hbm] * 13,
         out_specs=(vmem, vmem, vmem),
         scratch_shapes=[
             VMEM((4, rows, cols), BF16),
@@ -1026,6 +1073,10 @@
             VMEM((4, rows, cols), BF16),
             VMEM((2, 8, block), F32),
             VMEM((2, 3, 8, block), F32),
+            VMEM((rows, HEAD_DIM), F32),
+            VMEM((rows, HEAD_DIM), F32),
+            VMEM((2, rows, HEAD_DIM), F32),
+            VMEM((2, count, HEAD_DIM), F32),
             VMEM((group, rows, HEAD_DIM), BF16),
             VMEM((group, rows, HEAD_DIM), F32),
             VMEM((group, rows, HEAD_DIM), F32),
@@ -1034,7 +1085,7 @@
             VMEM((group, rows, HEAD_DIM), BF16),
             VMEM((group, 8, rows), F32),
             dma((PARTS,)),
-            dma((3,)),
+            dma((5,)),
             dma((4, 3)),
             dma((4,)),
             dma((6 * PARTS + 12,)),
@@ -1049,14 +1100,14 @@
             dma((2,)),
             dma((2,)),
             dma((2,)),
-            dma((2,)),
-            dma((2,)),
+            dma((3,)),
+            dma((3,)),
         ],
         compiler_params=pltpu.CompilerParams(
             collective_id=collective_id, has_side_effects=True, vmem_limit_bytes=50 * 2**20
         ),
         name="fused",
-    )(*far[:4], cos, sin, *far[4:])
+    )(*far)
 
 
 def finish_kernel(hid_ref, q_ref, kv_ref, hid_hbm, o_hbm, o_ref, sems):
@@ -1165,6 +1216,11 @@
 ):
     seq, tp = sizes
     rows, cols = tokens.shape
+    first = (query_weight, key_weight, value_weight)
+    second = (local_query_weight, local_key_weight, local_value_weight)
+    if tp == 4 and cols % HEAD_DIM == 0 and rows == 2 * WINDOW and seq % 2 == 0 and seq > 4:
+        gains = (attention_gain, post_gain, local_gain)
+        return finish(*fused(tokens, gains, first, output_weight, second, seq, 0))
     places = lax.axis_index("seq") * rows + lax.iota(jnp.int32, rows)
     halfway = HEAD_DIM // 2
     exponents = jnp.arange(halfway, dtype=F32) * (2.0 / HEAD_DIM)
@@ -1173,11 +1229,6 @@
     cosine, sine = jnp.cos(angles), jnp.sin(angles)
     cos = jnp.concatenate([cosine, cosine], axis=-1)
     sin = jnp.concatenate([-sine, sine], axis=-1)
-    first = (query_weight, key_weight, value_weight)
-    second = (local_query_weight, local_key_weight, local_value_weight)
-    if tp == 4 and cols % HEAD_DIM == 0 and rows == 2 * WINDOW and seq % 2 == 0 and seq > 4:
-        gains = (attention_gain, post_gain, local_gain)
-        return finish(*fused(tokens, gains, cos, sin, first, output_weight, second, seq, 0))
     lead = plain_gather_project(tokens, attention_gain, cos, sin, *first)
     attended = causal_attention(*lead, seq, 1)
     hidden = plain_output_project(attended, tokens, post_gain, output_weight)

time: 94.8 us -> 90.5 us (0.955)
  Pallas kernels: 93.1 us -> 89.5 us
    pallas_call x1, Pallas kernels: 91.3 us -> 87.7 us  [fused(): pl.pallas_call(functools.partial(fused_kernel, count // 2, heads, kv_head...]
where the time goes in v3:
time: 90.5 us; the launch traced here: 90.3 us
  Pallas kernels  89.5 us (99%)
    pallas_call x1, Pallas kernels, fused(): pl.pallas_call(functools.partial(fused_kernel, count // 2, heads, kv_head...  87.7 us

profile of v3, /device:TPU:24, one launch (start us, length us, event | category | flops | bytes accessed | tf_op | source)
XLA Modules:
  0.0 90.3 jit_solution(4237612702708493408)
XLA Ops:
  0.6 87.7 %fused.1 = (bf16[256,1152]{1,0:T(8,128)(2,1)S(1)}, bf16[8,256,128]{2,1,0:T(8,128)(2,1)S(1)}, bf16[2,4,384,128]{3,2,1,0:T(8,128)(2,1)S(1)}) custom-call(bf16[256,1152]{1,0:T(8,128)(2,1)} %x_hbm.1, f32[36,128]{1,0:T(8,128)} %bitcast.3, f32[36,128]{1,0:T(8,128)} %bitcast.4, f32[36,128]{1,0:T(8,128)} %bitcast.5, f32[2,256,128]{2,1,0:T(8,128)} %constant.4.clone.fine_hbm, ...), custom_call_target="tpu_custom_call" | custom-call | tf_op jit(solution)/shard_map/fused/pallas_call | solution.py:1046
  88.3 1.8 %finish.1 = (bf16[256,1152]{1,0:T(8,128)(2,1)}, bf16[256,1024]{1,0:T(8,128)(2,1)}) custom-call(bf16[256,1152]{1,0:T(8,128)(2,1)S(1)} %get-tuple-element.5.hid_ref, bf16[8,256,128]{2,1,0:T(8,128)(2,1)S(1)} %get-tuple-element.6.q_ref, bf16[2,4,384,128]{3,2,1,0:T(8,128)(2,1)S(1)} %get-tuple-element.7.kv_ref), custom_call_target="tpu_custom_call" | custom-call | tf_op jit(solution)/shard_map/finish/pallas_call | solution.py:1159

commit v4 on v3

--- a/solution.py
+++ b/solution.py
@@ -1,5 +1,6 @@
 import functools
 import math
+import types
 
 import jax
 import jax.numpy as jnp
@@ -21,6 +22,7 @@
 F32 = jnp.float32
 BF16 = jnp.bfloat16
 PARTS = 4
+HANDED = 16
 INNER = float(D // HEADS) ** (-0.5) / SOFT_CAP
 OUTER = SOFT_CAP * math.log2(math.e)
 
@@ -291,9 +293,12 @@
     wq_hbm, wk_hbm, wv_hbm, wo_hbm, lwq_hbm, lwk_hbm, lwv_hbm,
     hidden_ref, lq_ref, kv2,
     buf, w, wo, gains, xg, acc, ss, ss_first, q_all, kv_buf, out, lsum, att,
-    terms, own, landed, passed, proj, mine, stats, cos_ref, sin_ref, fine, coarse, q_up, out_up, lsum_up, up_num, up_sum, got_num, got_sum,
+    terms, own, landed, passed, proj, mine, stats, cos_ref, sin_ref, fine, coarse,
+    e_buf, e_att, e_terms, e_own, e_landed, e_passed, e_proj, e_xg, e_acc, e_ss, e_cos, e_sin,
+    e_hid, e_q, e_kv, r_hid, r_q, r_kv, q_up, out_up, lsum_up, up_num, up_sum, got_num, got_sum,
     x_sem, gain_sem, w_sem, wo_sem, ag_send, ag_recv, up_sem, side_sem, kv_sem,
-    rs_send, rs_recv, st_send, st_recv, tail_sem, down_send, down_recv, back_send, back_recv,
+    st_send, st_recv, tail_sem, down_send, down_recv, back_send, back_recv,
+    hand_send, hand_recv,
 ):
     me = lax.axis_index("tp")
     s = lax.axis_index("seq")
@@ -301,6 +306,8 @@
     mate = s + 1 - 2 * c
     has_up, has_down = z < levels - 1, z > 0
     top, helper = z == levels - 1, z == levels - 2
+    giver, taker = z >= levels // 2, z < levels // 2
+    partner = {"seq": 2 * (levels - 1 - z) + c}
     next_row, prev_row = s < 2 * levels - 1, s > 0
     rows, cols = hidden_ref.shape
     chunk_rows, half_rows = rows // PARTS, rows // PARTS // 2
@@ -398,20 +405,19 @@
     def moves(part):
         return gather_moves(buf, 0, chunk_rows, part, 0)
 
-    def moves2(part):
-        return gather_moves(proj, 6 * PARTS, block, part, 0)
-
     def kv_part(owner, part, count):
         here = pl.ds(pl.multiple_of(part * chunk_rows, chunk_rows), chunk_rows)
         return kv_buf.at[owner, :, pl.ds(0, count), here]
 
     def up(owner, part, count):
         at, ref = owner * PARTS + part, kv_part(owner, part, count)
-        return remote(ref, ref, up_sem.at[at], kv_sem.at[at], {"seq": s + 2})
+        held = owner // 2 * PARTS + part
+        return remote(ref, ref, up_sem.at[held], kv_sem.at[at], {"seq": s + 2})
 
     def side(owner, part, count):
         at, ref = owner * PARTS + part, kv_part(owner, part, count)
-        return remote(ref, ref, side_sem.at[at], kv_sem.at[at], {"seq": mate})
+        held = owner // 2 * PARTS + part
+        return remote(ref, ref, side_sem.at[held], kv_sem.at[at], {"seq": mate})
 
     def lift(owner, part, act):
         @pl.when(z < levels - 2)
@@ -514,6 +520,12 @@
         cosine, sine = coarse[0, pl.ds(s, 1), :], coarse[1, pl.ds(s, 1), :]
         cos_ref[span, :] = fine[0, span] * cosine - fine[1, span] * sine
         sin_ref[span, :] = fine[1, span] * cosine + fine[0, span] * sine
+    for i in range(2):
+        span = slice(i * HANDED, (i + 1) * HANDED)
+        here = slice(i * half, i * half + HANDED)
+        cosine, sine = coarse[0, pl.ds(partner["seq"], 1), :], coarse[1, pl.ds(partner["seq"], 1), :]
+        e_cos[span, :] = fine[0, here] * cosine - fine[1, here] * sine
+        e_sin[span, :] = fine[1, here] * cosine + fine[0, here] * sine
 
     def first_part(part, carry):
         with jax.named_scope("first_part"):
@@ -632,6 +644,20 @@
 
     lax.fori_loop(0, PARTS, first_part, 0)
     queries(1)
+
+    def hand(source, target, i):
+        return remote(source, target, hand_send.at[i], hand_recv.at[i], partner)
+
+    rows_given = [pl.ds(i * half, HANDED) for i in range(2)]
+    rows_taken = [pl.ds(i * HANDED, HANDED) for i in range(2)]
+    token_hands = [
+        hand(buf.at[:, rows_given[i]], e_buf.at[:, rows_taken[i]], i) for i in range(2)
+    ]
+    att_hands = [hand(att.at[rows_given[i]], e_att.at[rows_taken[i]], 2 + i) for i in range(2)]
+    returns = [
+        hand(source, target, 4 + i)
+        for i, (source, target) in enumerate(((e_hid, r_hid), (e_q, r_q), (e_kv, r_kv)))
+    ]
 
     second_loads = weight_loads(lwk_hbm, lwv_hbm, lwq_hbm)
 
@@ -778,130 +804,201 @@
             denominator = jnp.sum(lsum[h, span], axis=-1, keepdims=True)
             att[span, h * HEAD_DIM : (h + 1) * HEAD_DIM] = (out[h, span] / denominator).astype(BF16)
 
-    def reduce_moves(part):
-        base = part * block
-        top, bottom = pl.ds(base, half), pl.ds(base + half, half)
+    def own_piece(part):
+        return types.SimpleNamespace(
+            base=part * block, count=block, shared=part == 0, att=att, terms=terms, own=own,
+            landed=landed.at[part], passed=passed.at[part], proj=proj, tok=buf,
+            mine=mine.at[part], stats=stats.at[part], rs=part * 6, ag=18 + part * 6,
+            st=part * 3, xg=xg, acc=acc, ss=ss, cos=cos_ref, sin=sin_ref, hid=hidden_ref,
+            q=lq_ref, kv=kv2, kv_base=WINDOW + part * block,
+        )
+
+    soon, late = own_piece(1), own_piece(0)
+    extra = types.SimpleNamespace(
+        base=0, count=2 * HANDED, shared=False, att=e_att, terms=e_terms, own=e_own,
+        landed=e_landed, passed=e_passed, proj=e_proj, tok=e_buf, mine=mine.at[2],
+        stats=stats.at[2], rs=12, ag=30, st=6, xg=e_xg, acc=e_acc, ss=e_ss,
+        cos=e_cos, sin=e_sin, hid=e_hid, q=e_q, kv=e_kv, kv_base=0,
+    )
+
+    def reduce_moves(p, trim):
+        mid = p.count // 2
+        top_rows = pl.ds(p.base + trim, mid - trim)
+        low_rows = pl.ds(p.base + mid + trim, mid - trim)
+        cut = pl.ds(trim, mid - trim)
         spec = (
-            (terms.at[2, top], along_x),
-            (terms.at[2, bottom], along_y),
-            (terms.at[0, top], along_x),
-            (terms.at[1, bottom], along_y),
-            (passed.at[part, 1], along_x),
-            (passed.at[part, 0], along_y),
+            (p.terms.at[2, top_rows], along_x),
+            (p.terms.at[2, low_rows], along_y),
+            (p.terms.at[0, top_rows], along_x),
+            (p.terms.at[1, low_rows], along_y),
+            (p.passed.at[1, cut], along_x),
+            (p.passed.at[0, cut], along_y),
         )
         return [
             remote(
-                source, landed.at[part, i], rs_send.at[part * 6 + i], rs_recv.at[part * 6 + i], device
+                source, p.landed.at[i, cut], ag_send.at[p.rs + i], ag_recv.at[p.rs + i], device
             )
             for i, (source, device) in enumerate(spec)
         ]
 
-    def product(bits, part):
-        span = slice(part * block, (part + 1) * block)
-        value = jnp.dot(att[span, :], wo[bits], preferred_element_type=F32)
-        if bits == 0:
-            own[span, :] = value
-        else:
-            terms[bits - 1, span, :] = value.astype(BF16)
-
-    def pass_on(part):
-        copies = reduce_moves(part)
-        base = part * block
-        copies[0].wait_recv()
-        passed[part, 0] = (
-            terms[1, base : base + half].astype(F32) + landed[part, 0].astype(F32)
-        ).astype(BF16)
-        copies[5].start()
-        copies[1].wait_recv()
-        passed[part, 1] = (
-            terms[0, base + half : base + block].astype(F32) + landed[part, 1].astype(F32)
-        ).astype(BF16)
-        copies[4].start()
-
-    def swaps(part):
+    def gather2(p, trim):
+        mid = p.count // 2
+        top_rows = pl.ds(p.base + trim, mid - trim)
+        low_rows = pl.ds(p.base + mid + trim, mid - trim)
+        spec = (
+            (0, 1, top_rows, along_x),
+            (0, 2, low_rows, along_y),
+            (0, 1, low_rows, along_x),
+            (0, 2, top_rows, along_y),
+            (1, 3, top_rows, along_y),
+            (2, 3, low_rows, along_x),
+        )
         return [
             remote(
-                mine.at[part], stats.at[part, bits - 1],
-                st_send.at[part * 3 + bits - 1], st_recv.at[part * 3 + bits - 1], peers[bits],
+                p.proj.at[source, span], p.proj.at[target, span],
+                ag_send.at[p.ag + i], ag_recv.at[p.ag + i], device,
+            )
+            for i, (source, target, span, device) in enumerate(spec)
+        ]
+
+    def received(copy):
+        copy.wait_recv()
+
+    def each(make, p, picks, act):
+        def run(trim):
+            copies = make(p, trim)
+            for i in picks:
+                act(copies[i])
+
+        if p.shared:
+            pl.when(giver)(lambda: run(HANDED))
+            pl.when(taker)(lambda: run(0))
+        else:
+            run(0)
+
+    def product(bits, p):
+        span = slice(p.base, p.base + p.count)
+        value = jnp.dot(p.att[span, :], wo[bits], preferred_element_type=F32)
+        if bits == 0:
+            p.own[span, :] = value
+        else:
+            p.terms[bits - 1, span, :] = value.astype(BF16)
+
+    def send_products(p):
+        product(3, p)
+        each(reduce_moves, p, (0, 1), launch)
+        product(1, p)
+        each(reduce_moves, p, (2,), launch)
+        product(2, p)
+        each(reduce_moves, p, (3,), launch)
+        product(0, p)
+
+    def pass_on(p):
+        mid = p.count // 2
+        each(reduce_moves, p, (0,), received)
+        p.passed[0] = (
+            p.terms[1, p.base : p.base + mid].astype(F32) + p.landed[0].astype(F32)
+        ).astype(BF16)
+        each(reduce_moves, p, (5,), launch)
+        each(reduce_moves, p, (1,), received)
+        p.passed[1] = (
+            p.terms[0, p.base + mid : p.base + p.count].astype(F32) + p.landed[1].astype(F32)
+        ).astype(BF16)
+        each(reduce_moves, p, (4,), launch)
+
+    def swaps(p):
+        return [
+            remote(
+                p.mine, p.stats.at[bits - 1],
+                st_send.at[p.st + bits - 1], st_recv.at[p.st + bits - 1], peers[bits],
             )
             for bits in (3, 1, 2)
         ]
 
-    def finalize(part):
-        copies = reduce_moves(part)
-        for i in (2, 3, 5, 4):
-            copies[i].wait_recv()
-        base = part * block
-        span = slice(base, base + block)
+    def finalize(p):
+        each(reduce_moves, p, (2, 3, 5, 4), received)
+        span = slice(p.base, p.base + p.count)
         lanes = None
         for j in range(chunks):
             cut = slice(j * HEAD_DIM, (j + 1) * HEAD_DIM)
-            above = landed[part, 2, :, cut].astype(F32) + landed[part, 5, :, cut].astype(F32)
-            below = landed[part, 3, :, cut].astype(F32) + landed[part, 4, :, cut].astype(F32)
-            value = own[span, cut] + jnp.concatenate([above, below], axis=0)
-            own[span, cut] = value
-            proj[0, span, cut] = value.astype(BF16)
+            above = p.landed[2, :, cut].astype(F32) + p.landed[5, :, cut].astype(F32)
+            below = p.landed[3, :, cut].astype(F32) + p.landed[4, :, cut].astype(F32)
+            value = p.own[span, cut] + jnp.concatenate([above, below], axis=0)
+            p.own[span, cut] = value
+            p.proj[0, span, cut] = value.astype(BF16)
             lanes = value * value if lanes is None else lanes + value * value
-        for copy in moves2(part)[:2]:
-            copy.start()
-        mine[part] = lax.dot_general(
+        each(gather2, p, (0, 1), launch)
+        if p.count < block:
+            lanes = jnp.concatenate([lanes, jnp.zeros((block - p.count, HEAD_DIM), F32)], axis=0)
+        p.mine[...] = lax.dot_general(
             ones, lanes, (((1,), (1,)), ((), ())), precision=highest, preferred_element_type=F32
         )
-        for swap in swaps(part):
+        for swap in swaps(p):
             swap.start()
-        for copy in moves2(part)[2:4]:
-            copy.start()
-
-    def forward_rows(part):
-        copies = moves2(part)
-        copies[0].wait_recv()
-        copies[4].start()
-        copies[1].wait_recv()
-        copies[5].start()
-
-    def post_factor(part):
-        for swap in swaps(part):
+
+    def forward_rows(p):
+        each(gather2, p, (0,), received)
+        each(gather2, p, (4,), launch)
+        each(gather2, p, (1,), received)
+        each(gather2, p, (5,), launch)
+
+    def post_factor(p):
+        for swap in swaps(p):
             swap.wait_recv()
-        summed = mine[part] + stats[part, 0] + stats[part, 1] + stats[part, 2]
+        summed = p.mine[...] + p.stats[0] + p.stats[1] + p.stats[2]
         column = lax.dot_general(
             summed, ones * 0.125, (((0,), (0,)), ((), ())), precision=highest,
             preferred_element_type=F32,
         )
-        return lax.rsqrt(column * (1.0 / D) + NORM_EPS)
-
-    def take2(slot, part, factor):
-        span = slice(part * block, (part + 1) * block)
+        return lax.rsqrt(column[0 : p.count] * (1.0 / D) + NORM_EPS)
+
+    def take2(slot, p, factor):
+        arrivals = ((), (2,), (3,), (4, 5))[slot]
+        each(gather2, p, arrivals, received)
+        span = slice(p.base, p.base + p.count)
         squares = None
         for j in range(chunks):
             cut = slice(j * HEAD_DIM, (j + 1) * HEAD_DIM)
-            summed = own[span, cut] if slot == 0 else proj[slot, span, cut].astype(F32)
-            added = buf[slot, span, cut].astype(F32) + summed * factor * gain_row(1, slot, j)
+            summed = p.own[span, cut] if slot == 0 else p.proj[slot, span, cut].astype(F32)
+            added = p.tok[slot, span, cut].astype(F32) + summed * factor * gain_row(1, slot, j)
             rounded = added.astype(BF16)
             if slot == 0:
-                hidden_ref[span, cut] = rounded
+                p.hid[span, cut] = rounded
             wide = rounded.astype(F32)
             squares = wide * wide if squares is None else squares + wide * wide
-            xg[:, cut] = (wide * gain_row(2, slot, j)).astype(BF16)
+            p.xg[:, cut] = (wide * gain_row(2, slot, j)).astype(BF16)
         if slot == 0:
-            ss[...] = squares
+            p.ss[...] = squares
         else:
-            ss[...] += squares
-        if part == 1:
+            p.ss[...] += squares
+        if p is soon:
             for copy in second_loads[slot]:
                 copy.wait()
-        multiply(slot, block, 0, kvc, slot == 0)
-        multiply(slot, block, kvc, qc, slot == 0)
-
-    def finish2(part):
-        span = pl.ds(part * block, block)
-        place_rows = pl.ds(WINDOW + part * block, block)
-        factor = row_factor(ss[...])
+        for begin, width in ((0, kvc), (kvc, qc)):
+            value = jnp.dot(
+                p.xg[...], w[slot, :, begin : begin + width], preferred_element_type=F32
+            )
+            if slot == 0:
+                p.acc[:, begin : begin + width] = value
+            else:
+                p.acc[:, begin : begin + width] += value
+
+    def finish2(p):
+        span = slice(p.base, p.base + p.count)
+        place_rows = slice(p.kv_base, p.kv_base + p.count)
+        factor = row_factor(p.ss[...])
+
+        def spun(begin):
+            u = p.acc[:, begin : begin + HEAD_DIM] * factor
+            turned = pltpu.roll(u, HEAD_DIM // 2, 1)
+            return (u * p.cos[span, :] + turned * p.sin[span, :]).astype(BF16)
+
         for h in range(kv_heads):
-            kv2[0, h, place_rows, :] = rotated(h * HEAD_DIM, block, factor, span)
+            p.kv[0, h, place_rows, :] = spun(h * HEAD_DIM)
             place = kc + h * HEAD_DIM
-            kv2[1, h, place_rows, :] = (acc[:, place : place + HEAD_DIM] * factor).astype(BF16)
+            p.kv[1, h, place_rows, :] = (p.acc[:, place : place + HEAD_DIM] * factor).astype(BF16)
         for h in range(heads):
-            lq_ref[h, span, :] = rotated(kvc + h * HEAD_DIM, block, factor, span)
+            p.q[h, span, :] = spun(kvc + h * HEAD_DIM)
 
     tail = remote(
         kv2.at[:, :, pl.ds(rows, WINDOW)], kv2.at[:, :, pl.ds(0, WINDOW)],
@@ -912,41 +1009,105 @@
         with jax.named_scope(name):
             return run(*given)
 
+    def drain_early():
+        def drain_first(part, carry):
+            lift(s, part, sent)
+
+            @pl.when((c == 0) | helper)
+            def _():
+                side(s, part, kv_heads).wait_send()
+
+            def drain_level(k, carry):
+                lift(s - 2 * k, part, sent)
+
+                @pl.when(has_up)
+                def _():
+                    side(s - 2 * k, part, kv_heads).wait_send()
+
+                @pl.when(top)
+                def _():
+                    side(s - 2 * k, part, keep).wait_send()
+
+                return carry
+
+            lax.fori_loop(1, z + 1, drain_level, 0)
+            return carry
+
+        lax.fori_loop(0, PARTS, drain_first, 0)
+
+        @pl.when(helper)
+        def _():
+            for copy in backs:
+                copy.wait_send()
+
+        @pl.when(top)
+        def _():
+            for part in range(2):
+                query_down(part).wait_send()
+
+
+    def drain_pair(p):
+        each(reduce_moves, p, range(6), sent)
+        if p is not late:
+            each(gather2, p, range(6), sent)
+            for swap in swaps(p):
+                swap.wait_send()
+
     for copy in wo_loads:
         copy.wait()
-    late, soon = 0, 1
-    scoped("write_part", write_part, soon)
-    copies = reduce_moves(soon)
-    scoped("product", product, 3, soon)
-    copies[0].start()
-    copies[1].start()
-    scoped("product", product, 1, soon)
-    copies[2].start()
-    scoped("product", product, 2, soon)
-    copies[3].start()
-    scoped("product", product, 0, soon)
+
+    def drain_moves(part, carry):
+        for copy in moves(part):
+            copy.wait_send()
+
+        return carry
+
+    lax.fori_loop(0, PARTS, drain_moves, 0)
+    scoped("write_part", write_part, 1)
+    scoped("send_products", send_products, soon)
     fetch(0)
-    scoped("write_part", write_part, late)
+    scoped("write_part", write_part, 0)
+
+    @pl.when(giver)
+    def _():
+        for copy in (*att_hands, *token_hands):
+            copy.start()
+
     for bits in (3, 1, 2, 0):
-        scoped("product", product, bits, late)
+        product(bits, late)
     scoped("pass_on", pass_on, soon)
-    for copy in reduce_moves(late)[:4]:
-        copy.start()
+    each(reduce_moves, late, (0, 1, 2, 3), launch)
     fetch(1)
     fetch(2)
     fetch(3)
+    with jax.named_scope("early_drain"):
+        drain_early()
     scoped("finalize", finalize, soon)
+    each(gather2, soon, (2, 3), launch)
     scoped("pass_on", pass_on, late)
     factor = scoped("post_factor", post_factor, soon)
+
+    @pl.when(taker)
+    def _():
+        with jax.named_scope("extra_products"):
+            for copy in att_hands:
+                copy.wait_recv()
+            send_products(extra)
+
     scoped("take2", take2, 0, soon, factor)
     scoped("forward_rows", forward_rows, soon)
-    moves2(soon)[2].wait_recv()
     scoped("take2", take2, 1, soon, factor)
-    moves2(soon)[3].wait_recv()
     scoped("take2", take2, 2, soon, factor)
-    scoped("finalize", finalize, late)
-    moves2(soon)[4].wait_recv()
-    moves2(soon)[5].wait_recv()
+
+    @pl.when(giver)
+    def _():
+        scoped("finalize", finalize, late)
+        each(gather2, late, (2, 3), launch)
+
+    @pl.when(taker)
+    def _():
+        scoped("extra_pass_on", pass_on, extra)
+
     scoped("take2", take2, 3, soon, factor)
     scoped("finish2", finish2, soon)
 
@@ -958,63 +1119,77 @@
     def _():
         kv2[:, :, 0:WINDOW, :] = jnp.zeros((2, kv_heads, WINDOW, HEAD_DIM), BF16)
 
+    @pl.when(taker)
+    def _():
+        scoped("extra_finalize", finalize, extra)
+        each(gather2, extra, (2, 3), launch)
+        scoped("finalize", finalize, late)
+
+    drain_pair(soon)
+
+    @pl.when(giver)
+    def _():
+        for copy in (*token_hands, *att_hands):
+            copy.wait_send()
+
     factor = scoped("post_factor", post_factor, late)
     scoped("take2", take2, 0, late, factor)
+
+    @pl.when(taker)
+    def _():
+        scoped("extra_forward", forward_rows, extra)
+        each(gather2, late, (2, 3), launch)
+
     scoped("forward_rows", forward_rows, late)
-    moves2(late)[2].wait_recv()
+
+    @pl.when(taker)
+    def _():
+        with jax.named_scope("extra_take"):
+            extra_factor = post_factor(extra)
+            for copy in token_hands:
+                copy.wait_recv()
+            for slot in range(4):
+                take2(slot, extra, extra_factor)
+                if slot == 0:
+                    returns[0].start()
+            finish2(extra)
+            for copy in returns[1:]:
+                copy.start()
+            drain_pair(extra)
+
     scoped("take2", take2, 1, late, factor)
-    moves2(late)[3].wait_recv()
     scoped("take2", take2, 2, late, factor)
-    moves2(late)[4].wait_recv()
-    moves2(late)[5].wait_recv()
+    drain_pair(late)
     scoped("take2", take2, 3, late, factor)
     scoped("finish2", finish2, late)
 
+    @pl.when(giver)
+    def _():
+        with jax.named_scope("extra_return"):
+            for copy in returns:
+                copy.wait_recv()
+            for i in range(2):
+                here = slice(i * half, i * half + HANDED)
+                there = slice(i * HANDED, (i + 1) * HANDED)
+                kv_here = slice(WINDOW + i * half, WINDOW + i * half + HANDED)
+                hidden_ref[here, :] = r_hid[there, :]
+                lq_ref[:, here, :] = r_q[:, there, :]
+                kv2[:, :, kv_here, :] = r_kv[:, :, there, :]
+
     @pl.when(prev_row)
     def _():
-        tail.wait_recv()
-
-    def drain_first(part, carry):
-        for copy in moves(part):
-            copy.wait_send()
-
-        lift(s, part, sent)
-
-        @pl.when((c == 0) | helper)
-        def _():
-            side(s, part, kv_heads).wait_send()
-
-        def drain_level(k, carry):
-            lift(s - 2 * k, part, sent)
-
-            @pl.when(has_up)
-            def _():
-                side(s - 2 * k, part, kv_heads).wait_send()
-
-            @pl.when(top)
-            def _():
-                side(s - 2 * k, part, keep).wait_send()
-
-            return carry
-
-        lax.fori_loop(1, z + 1, drain_level, 0)
-        return carry
-
-    lax.fori_loop(0, PARTS, drain_first, 0)
-
-    @pl.when(helper)
-    def _():
-        for copy in backs:
-            copy.wait_send()
-
-    @pl.when(top)
-    def _():
-        for part in range(2):
-            query_down(part).wait_send()
-
-    for part in range(2):
-        for copy in (*reduce_moves(part), *swaps(part), *moves2(part)):
-            copy.wait_send()
+        with jax.named_scope("tail_wait"):
+            tail.wait_recv()
+
+    with jax.named_scope("drain"):
+        each(gather2, late, range(6), sent)
+        for swap in swaps(late):
+            swap.wait_send()
+
+        @pl.when(taker)
+        def _():
+            for copy in returns:
+                copy.wait_send()
 
     @pl.when(next_row)
     def _():
@@ -1027,7 +1202,7 @@
     heads, kv_heads = wq.shape[1] // HEAD_DIM, wk.shape[1] // HEAD_DIM
     total = wq.shape[1] + 2 * wk.shape[1]
     depth = wo.shape[0]
-    group, block = heads // kv_heads, rows // 2
+    group, block, extra = heads // kv_heads, rows // 2, 2 * HANDED
     vmem = pl.BlockSpec(memory_space=VMEM)
     hbm = pl.BlockSpec(memory_space=pltpu.HBM)
     dma = pltpu.SemaphoreType.DMA
@@ -1071,12 +1246,30 @@
             VMEM((2, 6, block // 2, cols), BF16),
             VMEM((2, 2, block // 2, cols), BF16),
             VMEM((4, rows, cols), BF16),
-            VMEM((2, 8, block), F32),
-            VMEM((2, 3, 8, block), F32),
+            VMEM((3, 8, block), F32),
+            VMEM((3, 3, 8, block), F32),
             VMEM((rows, HEAD_DIM), F32),
             VMEM((rows, HEAD_DIM), F32),
             VMEM((2, rows, HEAD_DIM), F32),
             VMEM((2, count, HEAD_DIM), F32),
+            VMEM((4, extra, cols), BF16),
+            VMEM((extra, depth), BF16),
+            VMEM((3, extra, cols), BF16),
+            VMEM((extra, cols), F32),
+            VMEM((6, HANDED, cols), BF16),
+            VMEM((2, HANDED, cols), BF16),
+            VMEM((4, extra, cols), BF16),
+            VMEM((extra, cols), BF16),
+            VMEM((extra, total), F32),
+            VMEM((extra, HEAD_DIM), F32),
+            VMEM((extra, HEAD_DIM), F32),
+            VMEM((extra, HEAD_DIM), F32),
+            VMEM((extra, cols), BF16),
+            VMEM((heads, extra, HEAD_DIM), BF16),
+            VMEM((2, kv_heads, extra, HEAD_DIM), BF16),
+            VMEM((extra, cols), BF16),
+            VMEM((heads, extra, HEAD_DIM), BF16),
+            VMEM((2, kv_heads, extra, HEAD_DIM), BF16),
             VMEM((group, rows, HEAD_DIM), BF16),
             VMEM((group, rows, HEAD_DIM), F32),
             VMEM((group, rows, HEAD_DIM), F32),
@@ -1088,20 +1281,20 @@
             dma((5,)),
             dma((4, 3)),
             dma((4,)),
-            dma((6 * PARTS + 12,)),
-            dma((6 * PARTS + 12,)),
+            dma((max(6 * PARTS, 36),)),
+            dma((max(6 * PARTS, 36),)),
+            dma((count // 2 * PARTS,)),
+            dma((count // 2 * PARTS,)),
             dma((count * PARTS,)),
-            dma((count * PARTS,)),
-            dma((count * PARTS,)),
-            dma((12,)),
-            dma((12,)),
-            dma((6,)),
-            dma((6,)),
+            dma((9,)),
+            dma((9,)),
             dma((2,)),
             dma((2,)),
             dma((2,)),
             dma((3,)),
             dma((3,)),
+            dma((7,)),
+            dma((7,)),
         ],
         compiler_params=pltpu.CompilerParams(
             collective_id=collective_id, has_side_effects=True, vmem_limit_bytes=50 * 2**20
@@ -1218,7 +1411,7 @@
     rows, cols = tokens.shape
     first = (query_weight, key_weight, value_weight)
     second = (local_query_weight, local_key_weight, local_value_weight)
-    if tp == 4 and cols % HEAD_DIM == 0 and rows == 2 * WINDOW and seq % 2 == 0 and seq > 4:
+    if tp == 4 and cols % HEAD_DIM == 0 and rows == 2 * WINDOW and seq % 4 == 0 and seq > 4:
         gains = (attention_gain, post_gain, local_gain)
         return finish(*fused(tokens, gains, first, output_weight, second, seq, 0))
     places = lax.axis_index("seq") * rows + lax.iota(jnp.int32, rows)

time: 90.5 us -> 86.3 us (0.954)
  Pallas kernels: 89.5 us -> 85.3 us
    pallas_call x1, Pallas kernels: 87.7 us -> 83.5 us  [fused(): pl.pallas_call(functools.partial(fused_kernel, count // 2, heads, kv_head...]
where the time goes in v4:
time: 86.3 us; the launch traced here: 86.1 us
  Pallas kernels  85.3 us (99%)
    pallas_call x1, Pallas kernels, fused(): pl.pallas_call(functools.partial(fused_kernel, count // 2, heads, kv_head...  83.5 us
    pallas_call x1, Pallas kernels, finish(): pl.pallas_call(finish_kernel, out_shape=(jax.ShapeDtypeStruct(hidden.shap...  1.79 us

profile of v4, /device:TPU:24, one launch (start us, length us, event | category | flops | bytes accessed | tf_op | source)
XLA Modules:
  0.0 86.1 jit_solution(13978858704611721090)
XLA Ops:
  0.6 83.5 %fused.1 = (bf16[256,1152]{1,0:T(8,128)(2,1)S(1)}, bf16[8,256,128]{2,1,0:T(8,128)(2,1)S(1)}, bf16[2,4,384,128]{3,2,1,0:T(8,128)(2,1)S(1)}) custom-call(bf16[256,1152]{1,0:T(8,128)(2,1)} %x_hbm.1, f32[36,128]{1,0:T(8,128)} %bitcast.3, f32[36,128]{1,0:T(8,128)} %bitcast.4, f32[36,128]{1,0:T(8,128)} %bitcast.5, f32[2,256,128]{2,1,0:T(8,128)} %constant.4.clone.fine_hbm, ...), custom_call_target="tpu_custom_call" | custom-call | tf_op jit(solution)/shard_map/fused/pallas_call | solution.py:1221
  84.2 1.8 %finish.1 = (bf16[256,1152]{1,0:T(8,128)(2,1)}, bf16[256,1024]{1,0:T(8,128)(2,1)}) custom-call(bf16[256,1152]{1,0:T(8,128)(2,1)S(1)} %get-tuple-element.5.hid_ref, bf16[8,256,128]{2,1,0:T(8,128)(2,1)S(1)} %get-tuple-element.6.q_ref, bf16[2,4,384,128]{3,2,1,0:T(8,128)(2,1)S(1)} %get-tuple-element.7.kv_ref), custom_call_target="tpu_custom_call" | custom-call | tf_op jit(solution)/shard_map/finish/pallas_call | solution.py:1352

commit v5 on v4

--- a/solution.py
+++ b/solution.py
@@ -295,8 +295,8 @@
     buf, w, wo, gains, xg, acc, ss, ss_first, q_all, kv_buf, out, lsum, att,
     terms, own, landed, passed, proj, mine, stats, cos_ref, sin_ref, fine, coarse,
     e_buf, e_att, e_terms, e_own, e_landed, e_passed, e_proj, e_xg, e_acc, e_ss, e_cos, e_sin,
-    e_hid, e_q, e_kv, r_hid, r_q, r_kv, q_up, out_up, lsum_up, up_num, up_sum, got_num, got_sum,
-    x_sem, gain_sem, w_sem, wo_sem, ag_send, ag_recv, up_sem, side_sem, kv_sem,
+    e_factor, e_hid, e_q, e_kv, r_hid, r_q, r_kv, q_up, out_up, lsum_up, up_num, up_sum, got_num, got_sum,
+    x_sem, gain_sem, w_sem, wo_sem, out_sem, ag_recv, up_sem, side_sem, kv_sem,
     st_send, st_recv, tail_sem, down_send, down_recv, back_send, back_recv,
     hand_send, hand_recv,
 ):
@@ -385,6 +385,9 @@
         4 + has_up.astype(jnp.int32) + has_down.astype(jnp.int32) + far.astype(jnp.int32),
     )
 
+    def all_sent(ref, sem):
+        remote(ref, ref, sem, sem, along_x).wait_send()
+
     def gather_moves(store, first, count, part, base):
         begin = pl.multiple_of(part * count, count)
         top, bottom = pl.ds(begin, count // 2), pl.ds(begin + count // 2, count // 2)
@@ -398,7 +401,7 @@
         )
         at = first + part * 6 + base
         return [
-            remote(source, target, ag_send.at[at + i], ag_recv.at[at + i], device)
+            remote(source, target, out_sem.at[part], ag_recv.at[at + i], device)
             for i, (source, target, device) in enumerate(spec)
         ]
 
@@ -410,14 +413,19 @@
         return kv_buf.at[owner, :, pl.ds(0, count), here]
 
     def up(owner, part, count):
-        at, ref = owner * PARTS + part, kv_part(owner, part, count)
-        held = owner // 2 * PARTS + part
-        return remote(ref, ref, up_sem.at[held], kv_sem.at[at], {"seq": s + 2})
+        at, ref = owner // 2 * PARTS + part, kv_part(owner, part, count)
+        return remote(ref, ref, up_sem.at[owner // 2], kv_sem.at[at], {"seq": s + 2})
 
     def side(owner, part, count):
-        at, ref = owner * PARTS + part, kv_part(owner, part, count)
-        held = owner // 2 * PARTS + part
-        return remote(ref, ref, side_sem.at[held], kv_sem.at[at], {"seq": mate})
+        at, ref = levels * PARTS + owner // 2, kv_part(owner, part, count)
+        return remote(ref, ref, side_sem.at[owner // 2], kv_sem.at[at], {"seq": mate})
+
+    def whole_block(owner, count):
+        return kv_buf.at[owner, :, pl.ds(0, count)]
+
+    def side_landed(owner, count):
+        ref, at = whole_block(owner, count), levels * PARTS + owner // 2
+        remote(ref, ref, side_sem.at[owner // 2], kv_sem.at[at], {"seq": mate}).wait_recv()
 
     def lift(owner, part, act):
         @pl.when(z < levels - 2)
@@ -712,8 +720,7 @@
 
     @pl.when(helper | (c == 1))
     def _():
-        for part in range(PARTS):
-            side(mate, part, kv_heads).wait_recv()
+        side_landed(mate, kv_heads)
 
     @pl.when(c == 1)
     def _():
@@ -752,8 +759,7 @@
                 @pl.when(helper)
                 def _():
                     visit_up(owner, False, whole)
-                    for p in range(PARTS):
-                        side(other, p, kv_heads).wait_recv()
+                    side_landed(other, kv_heads)
                     visit_up(other, False, whole)
 
                     @pl.when(k == z)
@@ -763,13 +769,11 @@
                 def both(j, carry):
                     @pl.when((j == 1) & top)
                     def _():
-                        for p in range(PARTS):
-                            side(other, p, keep).wait_recv()
+                        side_landed(other, keep)
 
                     @pl.when((j == 1) & (z < levels - 2))
                     def _():
-                        for p in range(PARTS):
-                            side(other, p, kv_heads).wait_recv()
+                        side_landed(other, kv_heads)
 
                     visit(owner + j * (other - owner), whole)
                     return carry
@@ -836,7 +840,7 @@
         )
         return [
             remote(
-                source, p.landed.at[i, cut], ag_send.at[p.rs + i], ag_recv.at[p.rs + i], device
+                source, p.landed.at[i, cut], out_sem.at[p.rs // 6], ag_recv.at[p.rs + i], device
             )
             for i, (source, device) in enumerate(spec)
         ]
@@ -856,7 +860,7 @@
         return [
             remote(
                 p.proj.at[source, span], p.proj.at[target, span],
-                ag_send.at[p.ag + i], ag_recv.at[p.ag + i], device,
+                out_sem.at[p.ag // 6], ag_recv.at[p.ag + i], device,
             )
             for i, (source, target, span, device) in enumerate(spec)
         ]
@@ -910,7 +914,7 @@
         return [
             remote(
                 p.mine, p.stats.at[bits - 1],
-                st_send.at[p.st + bits - 1], st_recv.at[p.st + bits - 1], peers[bits],
+                st_send.at[p.st // 3], st_recv.at[p.st + bits - 1], peers[bits],
             )
             for bits in (3, 1, 2)
         ]
@@ -1010,30 +1014,32 @@
             return run(*given)
 
     def drain_early():
-        def drain_first(part, carry):
-            lift(s, part, sent)
-
-            @pl.when((c == 0) | helper)
+        def drain_level(k, carry):
+            owner = s - 2 * k
+
+            @pl.when(z < levels - 2)
             def _():
-                side(s, part, kv_heads).wait_send()
-
-            def drain_level(k, carry):
-                lift(s - 2 * k, part, sent)
-
-                @pl.when(has_up)
-                def _():
-                    side(s - 2 * k, part, kv_heads).wait_send()
-
-                @pl.when(top)
-                def _():
-                    side(s - 2 * k, part, keep).wait_send()
-
-                return carry
-
-            lax.fori_loop(1, z + 1, drain_level, 0)
+                all_sent(whole_block(owner, kv_heads), up_sem.at[owner // 2])
+
+            @pl.when(helper)
+            def _():
+                all_sent(whole_block(owner, keep), up_sem.at[owner // 2])
+
+            @pl.when(has_up & ((k > 0) | (c == 0) | helper))
+            def _():
+                all_sent(whole_block(owner, kv_heads), side_sem.at[owner // 2])
+
+            @pl.when(top & (k > 0))
+            def _():
+                all_sent(whole_block(owner, keep), side_sem.at[owner // 2])
+
+            @pl.when(top & (k == 0) & (c == 0))
+            def _():
+                all_sent(whole_block(owner, kv_heads), side_sem.at[owner // 2])
+
             return carry
 
-        lax.fori_loop(0, PARTS, drain_first, 0)
+        lax.fori_loop(0, z + 1, drain_level, 0)
 
         @pl.when(helper)
         def _():
@@ -1046,20 +1052,29 @@
                 query_down(part).wait_send()
 
 
+    def drain_one(p, store, at):
+        def run(trim):
+            span = pl.ds(p.base, p.count - 2 * trim)
+            all_sent(store.at[pl.ds(0, 3), span], out_sem.at[at // 6])
+
+        if p.shared:
+            pl.when(giver)(lambda: run(HANDED))
+            pl.when(taker)(lambda: run(0))
+        else:
+            run(0)
+
     def drain_pair(p):
-        each(reduce_moves, p, range(6), sent)
+        drain_one(p, p.terms, p.rs)
         if p is not late:
-            each(gather2, p, range(6), sent)
-            for swap in swaps(p):
-                swap.wait_send()
+            drain_one(p, p.proj, p.ag)
+            all_sent(p.stats, st_send.at[p.st // 3])
 
     for copy in wo_loads:
         copy.wait()
 
     def drain_moves(part, carry):
-        for copy in moves(part):
-            copy.wait_send()
-
+        begin = pl.multiple_of(part * chunk_rows, chunk_rows)
+        all_sent(buf.at[pl.ds(0, 3), pl.ds(begin, chunk_rows)], out_sem.at[part])
         return carry
 
     lax.fori_loop(0, PARTS, drain_moves, 0)
@@ -1124,38 +1139,38 @@
         scoped("extra_finalize", finalize, extra)
         each(gather2, extra, (2, 3), launch)
         scoped("finalize", finalize, late)
-
-    drain_pair(soon)
-
-    @pl.when(giver)
-    def _():
-        for copy in (*token_hands, *att_hands):
-            copy.wait_send()
-
-    factor = scoped("post_factor", post_factor, late)
-    scoped("take2", take2, 0, late, factor)
-
-    @pl.when(taker)
-    def _():
         scoped("extra_forward", forward_rows, extra)
         each(gather2, late, (2, 3), launch)
-
-    scoped("forward_rows", forward_rows, late)
-
-    @pl.when(taker)
-    def _():
         with jax.named_scope("extra_take"):
-            extra_factor = post_factor(extra)
             for copy in token_hands:
                 copy.wait_recv()
-            for slot in range(4):
+            extra_factor = post_factor(extra)
+            for slot in range(3):
                 take2(slot, extra, extra_factor)
                 if slot == 0:
                     returns[0].start()
+            e_factor[...] = extra_factor
+
+    scoped("forward_rows", forward_rows, late)
+
+    @pl.when(taker)
+    def _():
+        with jax.named_scope("extra_last"):
+            take2(3, extra, e_factor[...])
             finish2(extra)
             for copy in returns[1:]:
                 copy.start()
             drain_pair(extra)
+
+    drain_pair(soon)
+
+    @pl.when(giver)
+    def _():
+        for copy in (*token_hands, *att_hands):
+            copy.wait_send()
+
+    factor = scoped("post_factor", post_factor, late)
+    scoped("take2", take2, 0, late, factor)
 
     scoped("take2", take2, 1, late, factor)
     scoped("take2", take2, 2, late, factor)
@@ -1182,9 +1197,8 @@
             tail.wait_recv()
 
     with jax.named_scope("drain"):
-        each(gather2, late, range(6), sent)
-        for swap in swaps(late):
-            swap.wait_send()
+        drain_one(late, proj, late.ag)
+        all_sent(late.stats, st_send.at[late.st // 3])
 
         @pl.when(taker)
         def _():
@@ -1264,6 +1278,7 @@
             VMEM((extra, HEAD_DIM), F32),
             VMEM((extra, HEAD_DIM), F32),
             VMEM((extra, HEAD_DIM), F32),
+            VMEM((extra, HEAD_DIM), F32),
             VMEM((extra, cols), BF16),
             VMEM((heads, extra, HEAD_DIM), BF16),
             VMEM((2, kv_heads, extra, HEAD_DIM), BF16),
@@ -1281,12 +1296,12 @@
             dma((5,)),
             dma((4, 3)),
             dma((4,)),
+            dma((6,)),
             dma((max(6 * PARTS, 36),)),
-            dma((max(6 * PARTS, 36),)),
-            dma((count // 2 * PARTS,)),
-            dma((count // 2 * PARTS,)),
-            dma((count * PARTS,)),
-            dma((9,)),
+            dma((count // 2,)),
+            dma((count // 2,)),
+            dma((count // 2 * (PARTS + 1),)),
+            dma((3,)),
             dma((9,)),
             dma((2,)),
             dma((2,)),

time: 86.3 us -> 84.5 us (0.979)
  Pallas kernels: 85.3 us -> 83.6 us
    pallas_call x1, Pallas kernels: 83.5 us -> 81.8 us  [fused(): pl.pallas_call(functools.partial(fused_kernel, count // 2, heads, kv_head...]
where the time goes in v5:
time: 84.5 us; the launch traced here: 84.4 us
  Pallas kernels  83.6 us (99%)
    pallas_call x1, Pallas kernels, fused(): pl.pallas_call(functools.partial(fused_kernel, count // 2, heads, kv_head...  81.8 us
    pallas_call x1, Pallas kernels, finish(): pl.pallas_call(finish_kernel, out_shape=(jax.ShapeDtypeStruct(hidden.shap...  1.79 us

profile of v5, /device:TPU:24, one launch (start us, length us, event | category | flops | bytes accessed | tf_op | source)
XLA Modules:
  0.0 84.4 jit_solution(2649372113367572064)
XLA Ops:
  0.6 81.8 %fused.1 = (bf16[256,1152]{1,0:T(8,128)(2,1)S(1)}, bf16[8,256,128]{2,1,0:T(8,128)(2,1)S(1)}, bf16[2,4,384,128]{3,2,1,0:T(8,128)(2,1)S(1)}) custom-call(bf16[256,1152]{1,0:T(8,128)(2,1)} %x_hbm.1, f32[36,128]{1,0:T(8,128)} %bitcast.3, f32[36,128]{1,0:T(8,128)} %bitcast.4, f32[36,128]{1,0:T(8,128)} %bitcast.5, f32[2,256,128]{2,1,0:T(8,128)} %constant.4.clone.fine_hbm, ...), custom_call_target="tpu_custom_call" | custom-call | tf_op jit(solution)/shard_map/fused/pallas_call | solution.py:1235
  82.4 1.8 %finish.1 = (bf16[256,1152]{1,0:T(8,128)(2,1)}, bf16[256,1024]{1,0:T(8,128)(2,1)}) custom-call(bf16[256,1152]{1,0:T(8,128)(2,1)S(1)} %get-tuple-element.5.hid_ref, bf16[8,256,128]{2,1,0:T(8,128)(2,1)S(1)} %get-tuple-element.6.q_ref, bf16[2,4,384,128]{3,2,1,0:T(8,128)(2,1)S(1)} %get-tuple-element.7.kv_ref), custom_call_target="tpu_custom_call" | custom-call | tf_op jit(solution)/shard_map/finish/pallas_call | solution.py:1367
